TPU v7x, 768 devices: a whole 4x8x12 slice. The times are simulated.
768 devices in a mesh: gx: 24 (over z, core), gy: 4 (over x), gz: 8 (over y).
Axes of the slice: x: 4, y: 8, z: 12, core: 2. Of those that a mesh axis runs over, the one named last changes fastest.
Arguments:
- residual: float32 [192, 32, 1024], P('gx', 'gy', 'gz'), may hold values from -18 to 18
- direction: float32 [192, 32, 1024], P('gx', 'gy', 'gz'), may hold values from -18 to 18
Outputs:
- powers: float32 [2, 4, 192, 32, 1024], P(None, None, 'gx', 'gy', 'gz')
- gram_matrix: float32 [9, 9], replicated
- projections: float32 [9], replicated
All inputs are finite; a program needn't handle non-finite values.
Results may differ from a plain program's by a relative error of at most 0.00029.
Values sent between devices are 32-bit elements; how exact they have to be, the bound alone decides.
No kernel may reach another device: no remote copies, remote signals or barrier semaphores. Data moves between devices by JAX's collectives and lax.ppermute only.
A program may use at most 32 MiB of HBM per device.

v0:
```python
import jax
import jax.numpy as jnp
from jax import lax
from jax.sharding import Mesh
from jax.sharding import PartitionSpec as P

STEPS = 4
MARGIN = 1
SWEEPS = 3
GX = ("gx_0", "gx_1")
GX_GY_GZ = ("gx_0", "gx_1", "gy", "gz")


SWEEP_SCALE = 1.0 / 9.0


def extended(cells, sides, width):
    for axis, dim in sides:
        count = lax.axis_size(axis)
        ends = count - 1
        head = lax.slice_in_dim(cells, 0, width, axis=dim)
        tail = lax.slice_in_dim(cells, cells.shape[dim] - width, cells.shape[dim], axis=dim)
        cells = jnp.concatenate(
            [
                lax.ppermute(tail, axis, [(i, (i + 1) % count) for i in range(ends)]),
                cells,
                lax.ppermute(head, axis, [((i + 1) % count, i) for i in range(ends)]),
            ],
            axis=dim,
        )
    return cells


def over_axes(x, axes):
    for axis in axes:
        x = lax.psum(x, axis)
    return x


def stencil_image(padded):
    center = padded[:, 1:-1, 1:-1, 1:-1]
    beside = padded[:, 2:, 1:-1, 1:-1] + padded[:, :-2, 1:-1, 1:-1]
    beside = beside + padded[:, 1:-1, 2:, 1:-1] + padded[:, 1:-1, :-2, 1:-1]
    beside = beside + padded[:, 1:-1, 1:-1, 2:] + padded[:, 1:-1, 1:-1, :-2]
    return 6.0 * center - beside


def pad_along(values, dimension, before, after):
    widths = [(0, 0)] * values.ndim
    widths[dimension] = (before, after)
    return jnp.pad(values, widths)


def assemble(received, reach, growth):
    for dimension in (1, 2, 3):
        length = received.shape[dimension] - 2 * reach
        result_len = length + 2 * growth
        middle = lax.slice_in_dim(received, reach, reach + length, axis=dimension)
        middle = pad_along(middle, dimension, growth, growth)
        below_part = lax.slice_in_dim(received, 0, reach, axis=dimension)
        above_part = lax.slice_in_dim(received, reach + length, 2 * reach + length, axis=dimension)
        received = (
            middle
            + pad_along(below_part, dimension, 0, result_len - reach)
            + pad_along(above_part, dimension, result_len - reach, 0)
        )
    return received


def inside_profile(position, cells, devices, margin):
    global_spots = position * cells - margin + jnp.arange(cells + 2 * margin, dtype=jnp.int32)
    return jnp.logical_and(global_spots >= 0, global_spots < devices * cells).astype(jnp.float32)


def grid_mask(cells_x, cells_y, cells_z, margin):
    along_x = inside_profile(lax.axis_index(GX), cells_x, lax.axis_size(GX), margin)
    along_y = inside_profile(lax.axis_index("gy"), cells_y, lax.axis_size("gy"), margin)
    along_z = inside_profile(lax.axis_index("gz"), cells_z, lax.axis_size("gz"), margin)
    return along_x[:, None, None] * along_y[None, :, None] * along_z[None, None, :]


def subdomain_solve(source, mask):
    source = mask * source
    iterate = mask * (SWEEP_SCALE * source)
    for sweep_index in range(SWEEPS - 1):
        padded = jnp.pad(iterate, ((0, 0), (1, 1), (1, 1), (1, 1)))
        iterate = mask * (iterate + SWEEP_SCALE * (source - stencil_image(padded)))
    return iterate


def flatten_rows(fields):
    return jnp.stack([member_field.reshape(-1) for member_field in fields])


def inner_table(left_rows, right_rows):
    return jnp.einsum("ac,bc->ab", left_rows, right_rows, precision=lax.Precision.HIGHEST)


def inner_vector(left_rows, target):
    return jnp.einsum("ac,c->a", left_rows, target, precision=lax.Precision.HIGHEST)


def local(residual, direction):
    margin = MARGIN
    cells_x, cells_y, cells_z = residual.shape
    mask = grid_mask(cells_x, cells_y, cells_z, margin)
    cell_count = float(
        lax.axis_size(GX) * cells_x * lax.axis_size("gy") * cells_y * lax.axis_size("gz") * cells_z
    )
    target = residual.reshape(-1)
    pieces = jnp.pad(
        jnp.stack([direction, residual]),
        ((0, 0), (margin, margin), (margin, margin), (margin, margin)),
    )
    p_fields, p_images, z_fields, z_images = ([], [], [], [])
    for step_index in range(STEPS + 1):
        final_step = step_index == STEPS
        source = None
        deep_reach = 2 * margin + 1
        received = extended(pieces, ((GX, 1), ("gy", 2), ("gz", 3)), deep_reach)
        region = assemble(received, deep_reach, 1)
        fields = region[
            :,
            margin + 1 : margin + 1 + cells_x,
            margin + 1 : margin + 1 + cells_y,
            margin + 1 : margin + 1 + cells_z,
        ]
        if final_step:
            own_images = stencil_image(
                region[
                    :,
                    margin : margin + cells_x + 2,
                    margin : margin + cells_y + 2,
                    margin : margin + cells_z + 2,
                ]
            )
        else:
            wide_images = stencil_image(region)
            own_images = wide_images[
                :, margin : margin + cells_x, margin : margin + cells_y, margin : margin + cells_z
            ]
            if step_index == 0:
                source = jnp.stack([wide_images[0], region[1, 1:-1, 1:-1, 1:-1]])
            else:
                source = wide_images
        p_fields.append(fields[0])
        p_images.append(own_images[0])
        if step_index > 0:
            z_fields.append(fields[1])
            z_images.append(own_images[1])
        if not final_step:
            pieces = subdomain_solve(source, mask)
    basis_rows = flatten_rows(p_fields + z_fields)
    image_rows = flatten_rows(p_images + z_images)
    gram_sum, projection_sum = (
        over_axes(inner_table(basis_rows, image_rows), GX_GY_GZ),
        over_axes(inner_vector(basis_rows, target), GX_GY_GZ),
    )
    powers = jnp.stack([jnp.stack(p_fields[1:]), jnp.stack(z_fields)])
    return (powers, gram_sum / cell_count, projection_sum / cell_count)


def solution(mesh):
    torus = Mesh(
        mesh.devices.reshape(12, 2, mesh.shape["gy"], mesh.shape["gz"]),
        ("gx_0", "gx_1", "gy", "gz"),
    )
    return jax.shard_map(
        local,
        mesh=torus,
        in_specs=(P(GX, "gy", "gz"), P(GX, "gy", "gz")),
        out_specs=(P(None, None, GX, "gy", "gz"), P(), P()),
        check_vma=False,
    )
```

profile of v0, /device:TPU:2, one launch (start us, length us, event | category | flops | bytes accessed | tf_op | source)
XLA Modules:
  0.0 236.8 jit_solution(11866736430806314737)
XLA Ops:
  4.7 3.9 %collective-permute-done.1 = f32[2,3,10,130]{3,2,1,0:T(8,128)S(1)} collective-permute-done((f32[2,3,10,130]{3,2,1,0:T(8,128)S(1)}, f32[2,3,10,130]{3,2,1,0:T(8,128)S(1)}, u32[]{:S(2)}, u32[]{:S(2)}) %collective-permute-start.1) | collective-permute-done | bytes 31232 | tf_op jit(solution)/shard_map/ppermute | solution.py:27
  8.7 3.4 %collective-permute-start.2 = (f32[2,16,3,130]{3,2,1,0:T(4,128)S(1)}, f32[2,16,3,130]{3,2,1,0:T(4,128)S(1)}, u32[]{:S(2)}, u32[]{:S(2)}) collective-permute-start(f32[2,16,3,130]{3,2,1,0:T(4,128)S(1)} %get-tuple-element.35), channel_id=1, source_target_pairs={{0,8},{8,16},{16,24},{1,9},{9,17},{17,25},{2,10},{10,18},{18,26},{... | collective-permute-start | bytes 149768 | tf_op jit(solution)/shard_map/ppermute | solution.py:25
  12.1 6.7 %collective-permute-start.3 = (f32[2,16,3,130]{3,2,1,0:T(4,128)S(1)}, f32[2,16,3,130]{3,2,1,0:T(4,128)S(1)}, u32[]{:S(2)}, u32[]{:S(2)}) collective-permute-start(f32[2,16,3,130]{3,2,1,0:T(4,128)S(1)} %get-tuple-element.36), channel_id=1, source_target_pairs={{8,0},{16,8},{24,16},{9,1},{17,9},{25,17},{10,2},{18,10},{26,18},{... | collective-permute-start | bytes 149768 | tf_op jit(solution)/shard_map/ppermute | solution.py:27
  24.9 5.2 %collective-permute-done.4 = f32[2,16,16,3]{3,2,1,0:T(8,128)S(1)} collective-permute-done((f32[2,16,16,3]{3,2,1,0:T(8,128)S(1)}, f32[2,16,16,3]{3,2,1,0:T(8,128)S(1)}, u32[]{:S(2)}, u32[]{:S(2)}) %collective-permute-start.4) | collective-permute-done | bytes 6176 | tf_op jit(solution)/shard_map/ppermute | solution.py:25
  30.1 4.4 %collective-permute-done.5 = f32[2,16,16,3]{3,2,1,0:T(8,128)S(1)} collective-permute-done((f32[2,16,16,3]{3,2,1,0:T(8,128)S(1)}, f32[2,16,16,3]{3,2,1,0:T(8,128)S(1)}, u32[]{:S(2)}, u32[]{:S(2)}) %collective-permute-start.5) | collective-permute-done | bytes 6176 | tf_op jit(solution)/shard_map/ppermute | solution.py:27
  41.5 4.0 %collective-permute-done.7 = f32[2,3,10,130]{3,2,1,0:T(8,128)S(1)} collective-permute-done((f32[2,3,10,130]{3,2,1,0:T(8,128)S(1)}, f32[2,3,10,130]{3,2,1,0:T(8,128)S(1)}, u32[]{:S(2)}, u32[]{:S(2)}) %collective-permute-start.7) | collective-permute-done | bytes 31232 | tf_op jit(solution)/shard_map/ppermute | solution.py:27
  45.5 3.1 %collective-permute-start.8 = (f32[2,16,3,130]{3,2,1,0:T(4,128)S(1)}, f32[2,16,3,130]{3,2,1,0:T(4,128)S(1)}, u32[]{:S(2)}, u32[]{:S(2)}) collective-permute-start(f32[2,16,3,130]{3,2,1,0:T(4,128)S(1)} %get-tuple-element.31), channel_id=1, source_target_pairs={{0,8},{8,16},{16,24},{1,9},{9,17},{17,25},{2,10},{10,18},{18,26},{... | collective-permute-start | bytes 149768 | tf_op jit(solution)/shard_map/ppermute | solution.py:25
  48.7 2.7 %collective-permute-start.9 = (f32[2,16,3,130]{3,2,1,0:T(4,128)S(1)}, f32[2,16,3,130]{3,2,1,0:T(4,128)S(1)}, u32[]{:S(2)}, u32[]{:S(2)}) collective-permute-start(f32[2,16,3,130]{3,2,1,0:T(4,128)S(1)} %get-tuple-element.32), channel_id=1, source_target_pairs={{8,0},{16,8},{24,16},{9,1},{17,9},{25,17},{10,2},{18,10},{26,18},{... | collective-permute-start | bytes 149768 | tf_op jit(solution)/shard_map/ppermute | solution.py:27
  52.4 3.1 %collective-permute-done.9 = f32[2,16,3,130]{3,2,1,0:T(4,128)S(1)} collective-permute-done((f32[2,16,3,130]{3,2,1,0:T(4,128)S(1)}, f32[2,16,3,130]{3,2,1,0:T(4,128)S(1)}, u32[]{:S(2)}, u32[]{:S(2)}) %collective-permute-start.9) | collective-permute-done | bytes 49952 | tf_op jit(solution)/shard_map/ppermute | solution.py:27
  55.8 3.5 %collective-permute-start.10 = (f32[2,16,16,3]{3,2,1,0:T(8,128)S(1)}, f32[2,16,16,3]{3,2,1,0:T(8,128)S(1)}, u32[]{:S(2)}, u32[]{:S(2)}) collective-permute-start(f32[2,16,16,3]{3,2,1,0:T(8,128)S(1)} %get-tuple-element.29), channel_id=1, source_target_pairs={{0,1},{1,2},{2,3},{3,4},{4,5},{5,6},{6,7},{8,9},{9,10},{10,11},{11... | collective-permute-start | bytes 18440 | tf_op jit(solution)/shard_map/ppermute | solution.py:25
  60.6 4.5 %collective-permute-done.10 = f32[2,16,16,3]{3,2,1,0:T(8,128)S(1)} collective-permute-done((f32[2,16,16,3]{3,2,1,0:T(8,128)S(1)}, f32[2,16,16,3]{3,2,1,0:T(8,128)S(1)}, u32[]{:S(2)}, u32[]{:S(2)}) %collective-permute-start.10) | collective-permute-done | bytes 6176 | tf_op jit(solution)/shard_map/ppermute | solution.py:25
  65.1 4.7 %collective-permute-done.11 = f32[2,16,16,3]{3,2,1,0:T(8,128)S(1)} collective-permute-done((f32[2,16,16,3]{3,2,1,0:T(8,128)S(1)}, f32[2,16,16,3]{3,2,1,0:T(8,128)S(1)}, u32[]{:S(2)}, u32[]{:S(2)}) %collective-permute-start.11) | collective-permute-done | bytes 6176 | tf_op jit(solution)/shard_map/ppermute | solution.py:27
  76.2 4.6 %collective-permute-done.13 = f32[2,3,10,130]{3,2,1,0:T(8,128)S(1)} collective-permute-done((f32[2,3,10,130]{3,2,1,0:T(8,128)S(1)}, f32[2,3,10,130]{3,2,1,0:T(8,128)S(1)}, u32[]{:S(2)}, u32[]{:S(2)}) %collective-permute-start.13) | collective-permute-done | bytes 31232 | tf_op jit(solution)/shard_map/ppermute | solution.py:27
  82.9 3.9 %collective-permute-start.15 = (f32[2,16,3,130]{3,2,1,0:T(4,128)S(1)}, f32[2,16,3,130]{3,2,1,0:T(4,128)S(1)}, u32[]{:S(2)}, u32[]{:S(2)}) collective-permute-start(f32[2,16,3,130]{3,2,1,0:T(4,128)S(1)} %get-tuple-element.28), channel_id=1, source_target_pairs={{8,0},{16,8},{24,16},{9,1},{17,9},{25,17},{10,2},{18,10},{26,18},{... | collective-permute-start | bytes 149768 | tf_op jit(solution)/shard_map/ppermute | solution.py:27
  90.0 5.2 %collective-permute-start.16 = (f32[2,16,16,3]{3,2,1,0:T(8,128)S(1)}, f32[2,16,16,3]{3,2,1,0:T(8,128)S(1)}, u32[]{:S(2)}, u32[]{:S(2)}) collective-permute-start(f32[2,16,16,3]{3,2,1,0:T(8,128)S(1)} %get-tuple-element.25), channel_id=1, source_target_pairs={{0,1},{1,2},{2,3},{3,4},{4,5},{5,6},{6,7},{8,9},{9,10},{10,11},{11... | collective-permute-start | bytes 18440 | tf_op jit(solution)/shard_map/ppermute | solution.py:25
  96.7 4.1 %collective-permute-done.16 = f32[2,16,16,3]{3,2,1,0:T(8,128)S(1)} collective-permute-done((f32[2,16,16,3]{3,2,1,0:T(8,128)S(1)}, f32[2,16,16,3]{3,2,1,0:T(8,128)S(1)}, u32[]{:S(2)}, u32[]{:S(2)}) %collective-permute-start.16) | collective-permute-done | bytes 6176 | tf_op jit(solution)/shard_map/ppermute | solution.py:25
  100.8 4.5 %collective-permute-done.17 = f32[2,16,16,3]{3,2,1,0:T(8,128)S(1)} collective-permute-done((f32[2,16,16,3]{3,2,1,0:T(8,128)S(1)}, f32[2,16,16,3]{3,2,1,0:T(8,128)S(1)}, u32[]{:S(2)}, u32[]{:S(2)}) %collective-permute-start.17) | collective-permute-done | bytes 6176 | tf_op jit(solution)/shard_map/ppermute | solution.py:27
  107.8 2.8 %collective-permute-start.18 = (f32[2,3,10,130]{3,2,1,0:T(8,128)S(1)}, f32[2,3,10,130]{3,2,1,0:T(8,128)S(1)}, u32[]{:S(2)}, u32[]{:S(2)}) collective-permute-start(f32[2,3,10,130]{3,2,1,0:T(8,128)S(1)} %get-tuple-element.53), channel_id=1, source_target_pairs={{0,32},{32,64},{64,96},{96,128},{128,160},{160,192},{192,224},{224... | collective-permute-start | bytes 93608 | tf_op jit(solution)/shard_map/ppermute | solution.py:25
  112.1 4.0 %collective-permute-done.19 = f32[2,3,10,130]{3,2,1,0:T(8,128)S(1)} collective-permute-done((f32[2,3,10,130]{3,2,1,0:T(8,128)S(1)}, f32[2,3,10,130]{3,2,1,0:T(8,128)S(1)}, u32[]{:S(2)}, u32[]{:S(2)}) %collective-permute-start.19) | collective-permute-done | bytes 31232 | tf_op jit(solution)/shard_map/ppermute | solution.py:27
  118.0 3.9 %collective-permute-start.21 = (f32[2,16,3,130]{3,2,1,0:T(4,128)S(1)}, f32[2,16,3,130]{3,2,1,0:T(4,128)S(1)}, u32[]{:S(2)}, u32[]{:S(2)}) collective-permute-start(f32[2,16,3,130]{3,2,1,0:T(4,128)S(1)} %get-tuple-element.24), channel_id=1, source_target_pairs={{8,0},{16,8},{24,16},{9,1},{17,9},{25,17},{10,2},{18,10},{26,18},{... | collective-permute-start | bytes 149768 | tf_op jit(solution)/shard_map/ppermute | solution.py:27
  125.2 4.2 %collective-permute-start.22 = (f32[2,16,16,3]{3,2,1,0:T(8,128)S(1)}, f32[2,16,16,3]{3,2,1,0:T(8,128)S(1)}, u32[]{:S(2)}, u32[]{:S(2)}) collective-permute-start(f32[2,16,16,3]{3,2,1,0:T(8,128)S(1)} %get-tuple-element.21), channel_id=1, source_target_pairs={{0,1},{1,2},{2,3},{3,4},{4,5},{5,6},{6,7},{8,9},{9,10},{10,11},{11... | collective-permute-start | bytes 18440 | tf_op jit(solution)/shard_map/ppermute | solution.py:25
  131.0 4.0 %collective-permute-done.22 = f32[2,16,16,3]{3,2,1,0:T(8,128)S(1)} collective-permute-done((f32[2,16,16,3]{3,2,1,0:T(8,128)S(1)}, f32[2,16,16,3]{3,2,1,0:T(8,128)S(1)}, u32[]{:S(2)}, u32[]{:S(2)}) %collective-permute-start.22) | collective-permute-done | bytes 6176 | tf_op jit(solution)/shard_map/ppermute | solution.py:25
  134.9 4.7 %collective-permute-done.23 = f32[2,16,16,3]{3,2,1,0:T(8,128)S(1)} collective-permute-done((f32[2,16,16,3]{3,2,1,0:T(8,128)S(1)}, f32[2,16,16,3]{3,2,1,0:T(8,128)S(1)}, u32[]{:S(2)}, u32[]{:S(2)}) %collective-permute-start.23) | collective-permute-done | bytes 6176 | tf_op jit(solution)/shard_map/ppermute | solution.py:27
  142.2 2.6 %collective-permute-start.24 = (f32[2,3,10,130]{3,2,1,0:T(8,128)S(1)}, f32[2,3,10,130]{3,2,1,0:T(8,128)S(1)}, u32[]{:S(2)}, u32[]{:S(2)}) collective-permute-start(f32[2,3,10,130]{3,2,1,0:T(8,128)S(1)} %get-tuple-element.51), channel_id=1, source_target_pairs={{0,32},{32,64},{64,96},{96,128},{128,160},{160,192},{192,224},{224... | collective-permute-start | bytes 93608 | tf_op jit(solution)/shard_map/ppermute | solution.py:25
  146.2 4.1 %collective-permute-done.25 = f32[2,3,10,130]{3,2,1,0:T(8,128)S(1)} collective-permute-done((f32[2,3,10,130]{3,2,1,0:T(8,128)S(1)}, f32[2,3,10,130]{3,2,1,0:T(8,128)S(1)}, u32[]{:S(2)}, u32[]{:S(2)}) %collective-permute-start.25) | collective-permute-done | bytes 31232 | tf_op jit(solution)/shard_map/ppermute | solution.py:27
  152.3 3.9 %collective-permute-start.27 = (f32[2,16,3,130]{3,2,1,0:T(4,128)S(1)}, f32[2,16,3,130]{3,2,1,0:T(4,128)S(1)}, u32[]{:S(2)}, u32[]{:S(2)}) collective-permute-start(f32[2,16,3,130]{3,2,1,0:T(4,128)S(1)} %get-tuple-element.20), channel_id=1, source_target_pairs={{8,0},{16,8},{24,16},{9,1},{17,9},{25,17},{10,2},{18,10},{26,18},{... | collective-permute-start | bytes 149768 | tf_op jit(solution)/shard_map/ppermute | solution.py:27
  159.5 2.9 %collective-permute-start.28 = (f32[2,16,16,3]{3,2,1,0:T(8,128)S(1)}, f32[2,16,16,3]{3,2,1,0:T(8,128)S(1)}, u32[]{:S(2)}, u32[]{:S(2)}) collective-permute-start(f32[2,16,16,3]{3,2,1,0:T(8,128)S(1)} %get-tuple-element.17), channel_id=1, source_target_pairs={{0,1},{1,2},{2,3},{3,4},{4,5},{5,6},{6,7},{8,9},{9,10},{10,11},{11... | collective-permute-start | bytes 18440 | tf_op jit(solution)/shard_map/ppermute | solution.py:25
  163.8 4.2 %collective-permute-done.28 = f32[2,16,16,3]{3,2,1,0:T(8,128)S(1)} collective-permute-done((f32[2,16,16,3]{3,2,1,0:T(8,128)S(1)}, f32[2,16,16,3]{3,2,1,0:T(8,128)S(1)}, u32[]{:S(2)}, u32[]{:S(2)}) %collective-permute-start.28) | collective-permute-done | bytes 6176 | tf_op jit(solution)/shard_map/ppermute | solution.py:25
  167.9 4.7 %collective-permute-done.29 = f32[2,16,16,3]{3,2,1,0:T(8,128)S(1)} collective-permute-done((f32[2,16,16,3]{3,2,1,0:T(8,128)S(1)}, f32[2,16,16,3]{3,2,1,0:T(8,128)S(1)}, u32[]{:S(2)}, u32[]{:S(2)}) %collective-permute-start.29) | collective-permute-done | bytes 6176 | tf_op jit(solution)/shard_map/ppermute | solution.py:27
  176.7 29.8 %all-reduce.39 = (f32[9,9]{1,0:T(8,128)S(1)}, f32[9]{0:T(128)S(1)}) all-reduce(f32[9,9]{1,0:T(8,128)S(1)} %fusion.151, f32[9]{0:T(128)S(1)} %convolution_bitcast_fusion), channel_id=1, replica_groups=mesh['gx_0'=12,'gx_1'=2,'gy'=4,'gz'=8] {'gx_0'}, use_global_device_ids=true, to_apply=%region_0.1 | all-reduce | flops 90 | bytes 720 | tf_op jit(solution)/shard_map/psum | solution.py:36
  209.1 10.0 %all-reduce.41 = (f32[9,9]{1,0:T(8,128)S(1)}, f32[9]{0:T(128)S(1)}) all-reduce(f32[9,9]{1,0:T(8,128)S(1)} %get-tuple-element.9, f32[9]{0:T(128)S(1)} %get-tuple-element.10), channel_id=1, replica_groups=mesh['gx_0'=12,'gx_1'=2,'gy'=4,'gz'=8] {'gy'}, use_global_device_ids=true, to_apply=%region_2.3 | all-reduce | flops 90 | bytes 720 | tf_op jit(solution)/shard_map/psum | solution.py:36
  219.0 16.0 %all-reduce.40 = (f32[9,9]{1,0:T(8,128)S(1)}, f32[9]{0:T(128)S(1)}) all-reduce(f32[9,9]{1,0:T(8,128)S(1)} %get-tuple-element.7, f32[9]{0:T(128)S(1)} %get-tuple-element.8), channel_id=1, replica_groups=mesh['gx_0'=12,'gx_1'=2,'gy'=4,'gz'=8] {'gz'}, use_global_device_ids=true, to_apply=%region_3.4 | all-reduce | flops 90 | bytes 720 | tf_op jit(solution)/shard_map/psum | solution.py:36
  (143 shorter events, 62.0 us)
Async XLA Ops:
  1.6 3.2 %collective-permute-start = (f32[2,3,10,130]{3,2,1,0:T(8,128)S(1)}, f32[2,3,10,130]{3,2,1,0:T(8,128)S(1)}, u32[]{:S(2)}, u32[]{:S(2)}) collective-permute-start(f32[2,3,10,130]{3,2,1,0:T(8,128)S(1)} %get-tuple-element.59), channel_id=1, source_target_pairs={{0,32},{32,64},{64,96},{96,128},{128,160},{160,192},{192,224},{224... | collective-permute-start | bytes 93608 | tf_op jit(solution)/shard_map/ppermute | solution.py:25
  3.3 5.3 %collective-permute-start.1 = (f32[2,3,10,130]{3,2,1,0:T(8,128)S(1)}, f32[2,3,10,130]{3,2,1,0:T(8,128)S(1)}, u32[]{:S(2)}, u32[]{:S(2)}) collective-permute-start(f32[2,3,10,130]{3,2,1,0:T(8,128)S(1)} %get-tuple-element.60), channel_id=1, source_target_pairs={{32,0},{64,32},{96,64},{128,96},{160,128},{192,160},{224,192},{256... | collective-permute-start | bytes 93608 | tf_op jit(solution)/shard_map/ppermute | solution.py:27
  8.7 12.0 %collective-permute-start.2 = (f32[2,16,3,130]{3,2,1,0:T(4,128)S(1)}, f32[2,16,3,130]{3,2,1,0:T(4,128)S(1)}, u32[]{:S(2)}, u32[]{:S(2)}) collective-permute-start(f32[2,16,3,130]{3,2,1,0:T(4,128)S(1)} %get-tuple-element.35), channel_id=1, source_target_pairs={{0,8},{8,16},{16,24},{1,9},{9,17},{17,25},{2,10},{10,18},{18,26},{... | collective-permute-start | bytes 149768 | tf_op jit(solution)/shard_map/ppermute | solution.py:25
  12.1 9.8 %collective-permute-start.3 = (f32[2,16,3,130]{3,2,1,0:T(4,128)S(1)}, f32[2,16,3,130]{3,2,1,0:T(4,128)S(1)}, u32[]{:S(2)}, u32[]{:S(2)}) collective-permute-start(f32[2,16,3,130]{3,2,1,0:T(4,128)S(1)} %get-tuple-element.36), channel_id=1, source_target_pairs={{8,0},{16,8},{24,16},{9,1},{17,9},{25,17},{10,2},{18,10},{26,18},{... | collective-permute-start | bytes 149768 | tf_op jit(solution)/shard_map/ppermute | solution.py:27
  22.2 7.9 %collective-permute-start.4 = (f32[2,16,16,3]{3,2,1,0:T(8,128)S(1)}, f32[2,16,16,3]{3,2,1,0:T(8,128)S(1)}, u32[]{:S(2)}, u32[]{:S(2)}) collective-permute-start(f32[2,16,16,3]{3,2,1,0:T(8,128)S(1)} %get-tuple-element.33), channel_id=1, source_target_pairs={{0,1},{1,2},{2,3},{3,4},{4,5},{5,6},{6,7},{8,9},{9,10},{10,11},{11... | collective-permute-start | bytes 18440 | tf_op jit(solution)/shard_map/ppermute | solution.py:25
  23.5 10.9 %collective-permute-start.5 = (f32[2,16,16,3]{3,2,1,0:T(8,128)S(1)}, f32[2,16,16,3]{3,2,1,0:T(8,128)S(1)}, u32[]{:S(2)}, u32[]{:S(2)}) collective-permute-start(f32[2,16,16,3]{3,2,1,0:T(8,128)S(1)} %get-tuple-element.34), channel_id=1, source_target_pairs={{1,0},{2,1},{3,2},{4,3},{5,4},{6,5},{7,6},{9,8},{10,9},{11,10},{12... | collective-permute-start | bytes 18440 | tf_op jit(solution)/shard_map/ppermute | solution.py:27
  36.0 0.7 copy-start.2
  38.3 3.2 %collective-permute-start.6 = (f32[2,3,10,130]{3,2,1,0:T(8,128)S(1)}, f32[2,3,10,130]{3,2,1,0:T(8,128)S(1)}, u32[]{:S(2)}, u32[]{:S(2)}) collective-permute-start(f32[2,3,10,130]{3,2,1,0:T(8,128)S(1)} %get-tuple-element.57), channel_id=1, source_target_pairs={{0,32},{32,64},{64,96},{96,128},{128,160},{160,192},{192,224},{224... | collective-permute-start | bytes 93608 | tf_op jit(solution)/shard_map/ppermute | solution.py:25
  40.2 5.3 %collective-permute-start.7 = (f32[2,3,10,130]{3,2,1,0:T(8,128)S(1)}, f32[2,3,10,130]{3,2,1,0:T(8,128)S(1)}, u32[]{:S(2)}, u32[]{:S(2)}) collective-permute-start(f32[2,3,10,130]{3,2,1,0:T(8,128)S(1)} %get-tuple-element.58), channel_id=1, source_target_pairs={{32,0},{64,32},{96,64},{128,96},{160,128},{192,160},{224,192},{256... | collective-permute-start | bytes 93608 | tf_op jit(solution)/shard_map/ppermute | solution.py:27
  45.5 6.9 %collective-permute-start.8 = (f32[2,16,3,130]{3,2,1,0:T(4,128)S(1)}, f32[2,16,3,130]{3,2,1,0:T(4,128)S(1)}, u32[]{:S(2)}, u32[]{:S(2)}) collective-permute-start(f32[2,16,3,130]{3,2,1,0:T(4,128)S(1)} %get-tuple-element.31), channel_id=1, source_target_pairs={{0,8},{8,16},{16,24},{1,9},{9,17},{17,25},{2,10},{10,18},{18,26},{... | collective-permute-start | bytes 149768 | tf_op jit(solution)/shard_map/ppermute | solution.py:25
  48.7 6.9 %collective-permute-start.9 = (f32[2,16,3,130]{3,2,1,0:T(4,128)S(1)}, f32[2,16,3,130]{3,2,1,0:T(4,128)S(1)}, u32[]{:S(2)}, u32[]{:S(2)}) collective-permute-start(f32[2,16,3,130]{3,2,1,0:T(4,128)S(1)} %get-tuple-element.32), channel_id=1, source_target_pairs={{8,0},{16,8},{24,16},{9,1},{17,9},{25,17},{10,2},{18,10},{26,18},{... | collective-permute-start | bytes 149768 | tf_op jit(solution)/shard_map/ppermute | solution.py:27
  55.8 9.3 %collective-permute-start.10 = (f32[2,16,16,3]{3,2,1,0:T(8,128)S(1)}, f32[2,16,16,3]{3,2,1,0:T(8,128)S(1)}, u32[]{:S(2)}, u32[]{:S(2)}) collective-permute-start(f32[2,16,16,3]{3,2,1,0:T(8,128)S(1)} %get-tuple-element.29), channel_id=1, source_target_pairs={{0,1},{1,2},{2,3},{3,4},{4,5},{5,6},{6,7},{8,9},{9,10},{10,11},{11... | collective-permute-start | bytes 18440 | tf_op jit(solution)/shard_map/ppermute | solution.py:25
  59.3 10.5 %collective-permute-start.11 = (f32[2,16,16,3]{3,2,1,0:T(8,128)S(1)}, f32[2,16,16,3]{3,2,1,0:T(8,128)S(1)}, u32[]{:S(2)}, u32[]{:S(2)}) collective-permute-start(f32[2,16,16,3]{3,2,1,0:T(8,128)S(1)} %get-tuple-element.30), channel_id=1, source_target_pairs={{1,0},{2,1},{3,2},{4,3},{5,4},{6,5},{7,6},{9,8},{10,9},{11,10},{12... | collective-permute-start | bytes 18440 | tf_op jit(solution)/shard_map/ppermute | solution.py:27
  72.4 3.9 %collective-permute-start.12 = (f32[2,3,10,130]{3,2,1,0:T(8,128)S(1)}, f32[2,3,10,130]{3,2,1,0:T(8,128)S(1)}, u32[]{:S(2)}, u32[]{:S(2)}) collective-permute-start(f32[2,3,10,130]{3,2,1,0:T(8,128)S(1)} %get-tuple-element.55), channel_id=1, source_target_pairs={{0,32},{32,64},{64,96},{96,128},{128,160},{160,192},{192,224},{224... | collective-permute-start | bytes 93608 | tf_op jit(solution)/shard_map/ppermute | solution.py:25
  74.9 5.9 %collective-permute-start.13 = (f32[2,3,10,130]{3,2,1,0:T(8,128)S(1)}, f32[2,3,10,130]{3,2,1,0:T(8,128)S(1)}, u32[]{:S(2)}, u32[]{:S(2)}) collective-permute-start(f32[2,3,10,130]{3,2,1,0:T(8,128)S(1)} %get-tuple-element.56), channel_id=1, source_target_pairs={{32,0},{64,32},{96,64},{128,96},{160,128},{192,160},{224,192},{256... | collective-permute-start | bytes 93608 | tf_op jit(solution)/shard_map/ppermute | solution.py:27
  80.9 6.9 %collective-permute-start.14 = (f32[2,16,3,130]{3,2,1,0:T(4,128)S(1)}, f32[2,16,3,130]{3,2,1,0:T(4,128)S(1)}, u32[]{:S(2)}, u32[]{:S(2)}) collective-permute-start(f32[2,16,3,130]{3,2,1,0:T(4,128)S(1)} %get-tuple-element.27), channel_id=1, source_target_pairs={{0,8},{8,16},{16,24},{1,9},{9,17},{17,25},{2,10},{10,18},{18,26},{... | collective-permute-start | bytes 149768 | tf_op jit(solution)/shard_map/ppermute | solution.py:25
  82.9 6.9 %collective-permute-start.15 = (f32[2,16,3,130]{3,2,1,0:T(4,128)S(1)}, f32[2,16,3,130]{3,2,1,0:T(4,128)S(1)}, u32[]{:S(2)}, u32[]{:S(2)}) collective-permute-start(f32[2,16,3,130]{3,2,1,0:T(4,128)S(1)} %get-tuple-element.28), channel_id=1, source_target_pairs={{8,0},{16,8},{24,16},{9,1},{17,9},{25,17},{10,2},{18,10},{26,18},{... | collective-permute-start | bytes 149768 | tf_op jit(solution)/shard_map/ppermute | solution.py:27
  90.0 10.8 %collective-permute-start.16 = (f32[2,16,16,3]{3,2,1,0:T(8,128)S(1)}, f32[2,16,16,3]{3,2,1,0:T(8,128)S(1)}, u32[]{:S(2)}, u32[]{:S(2)}) collective-permute-start(f32[2,16,16,3]{3,2,1,0:T(8,128)S(1)} %get-tuple-element.25), channel_id=1, source_target_pairs={{0,1},{1,2},{2,3},{3,4},{4,5},{5,6},{6,7},{8,9},{9,10},{10,11},{11... | collective-permute-start | bytes 18440 | tf_op jit(solution)/shard_map/ppermute | solution.py:25
  95.2 10.0 %collective-permute-start.17 = (f32[2,16,16,3]{3,2,1,0:T(8,128)S(1)}, f32[2,16,16,3]{3,2,1,0:T(8,128)S(1)}, u32[]{:S(2)}, u32[]{:S(2)}) collective-permute-start(f32[2,16,16,3]{3,2,1,0:T(8,128)S(1)} %get-tuple-element.26), channel_id=1, source_target_pairs={{1,0},{2,1},{3,2},{4,3},{5,4},{6,5},{7,6},{9,8},{10,9},{11,10},{12... | collective-permute-start | bytes 18440 | tf_op jit(solution)/shard_map/ppermute | solution.py:27
  107.8 4.2 %collective-permute-start.18 = (f32[2,3,10,130]{3,2,1,0:T(8,128)S(1)}, f32[2,3,10,130]{3,2,1,0:T(8,128)S(1)}, u32[]{:S(2)}, u32[]{:S(2)}) collective-permute-start(f32[2,3,10,130]{3,2,1,0:T(8,128)S(1)} %get-tuple-element.53), channel_id=1, source_target_pairs={{0,32},{32,64},{64,96},{96,128},{128,160},{160,192},{192,224},{224... | collective-permute-start | bytes 93608 | tf_op jit(solution)/shard_map/ppermute | solution.py:25
  110.7 5.4 %collective-permute-start.19 = (f32[2,3,10,130]{3,2,1,0:T(8,128)S(1)}, f32[2,3,10,130]{3,2,1,0:T(8,128)S(1)}, u32[]{:S(2)}, u32[]{:S(2)}) collective-permute-start(f32[2,3,10,130]{3,2,1,0:T(8,128)S(1)} %get-tuple-element.54), channel_id=1, source_target_pairs={{32,0},{64,32},{96,64},{128,96},{160,128},{192,160},{224,192},{256... | collective-permute-start | bytes 93608 | tf_op jit(solution)/shard_map/ppermute | solution.py:27
  116.1 6.9 %collective-permute-start.20 = (f32[2,16,3,130]{3,2,1,0:T(4,128)S(1)}, f32[2,16,3,130]{3,2,1,0:T(4,128)S(1)}, u32[]{:S(2)}, u32[]{:S(2)}) collective-permute-start(f32[2,16,3,130]{3,2,1,0:T(4,128)S(1)} %get-tuple-element.23), channel_id=1, source_target_pairs={{0,8},{8,16},{16,24},{1,9},{9,17},{17,25},{2,10},{10,18},{18,26},{... | collective-permute-start | bytes 149768 | tf_op jit(solution)/shard_map/ppermute | solution.py:25
  118.0 6.9 %collective-permute-start.21 = (f32[2,16,3,130]{3,2,1,0:T(4,128)S(1)}, f32[2,16,3,130]{3,2,1,0:T(4,128)S(1)}, u32[]{:S(2)}, u32[]{:S(2)}) collective-permute-start(f32[2,16,3,130]{3,2,1,0:T(4,128)S(1)} %get-tuple-element.24), channel_id=1, source_target_pairs={{8,0},{16,8},{24,16},{9,1},{17,9},{25,17},{10,2},{18,10},{26,18},{... | collective-permute-start | bytes 149768 | tf_op jit(solution)/shard_map/ppermute | solution.py:27
  125.2 9.8 %collective-permute-start.22 = (f32[2,16,16,3]{3,2,1,0:T(8,128)S(1)}, f32[2,16,16,3]{3,2,1,0:T(8,128)S(1)}, u32[]{:S(2)}, u32[]{:S(2)}) collective-permute-start(f32[2,16,16,3]{3,2,1,0:T(8,128)S(1)} %get-tuple-element.21), channel_id=1, source_target_pairs={{0,1},{1,2},{2,3},{3,4},{4,5},{5,6},{6,7},{8,9},{9,10},{10,11},{11... | collective-permute-start | bytes 18440 | tf_op jit(solution)/shard_map/ppermute | solution.py:25
  129.4 10.2 %collective-permute-start.23 = (f32[2,16,16,3]{3,2,1,0:T(8,128)S(1)}, f32[2,16,16,3]{3,2,1,0:T(8,128)S(1)}, u32[]{:S(2)}, u32[]{:S(2)}) collective-permute-start(f32[2,16,16,3]{3,2,1,0:T(8,128)S(1)} %get-tuple-element.22), channel_id=1, source_target_pairs={{1,0},{2,1},{3,2},{4,3},{5,4},{6,5},{7,6},{9,8},{10,9},{11,10},{12... | collective-permute-start | bytes 18440 | tf_op jit(solution)/shard_map/ppermute | solution.py:27
  142.2 4.0 %collective-permute-start.24 = (f32[2,3,10,130]{3,2,1,0:T(8,128)S(1)}, f32[2,3,10,130]{3,2,1,0:T(8,128)S(1)}, u32[]{:S(2)}, u32[]{:S(2)}) collective-permute-start(f32[2,3,10,130]{3,2,1,0:T(8,128)S(1)} %get-tuple-element.51), channel_id=1, source_target_pairs={{0,32},{32,64},{64,96},{96,128},{128,160},{160,192},{192,224},{224... | collective-permute-start | bytes 93608 | tf_op jit(solution)/shard_map/ppermute | solution.py:25
  144.8 5.5 %collective-permute-start.25 = (f32[2,3,10,130]{3,2,1,0:T(8,128)S(1)}, f32[2,3,10,130]{3,2,1,0:T(8,128)S(1)}, u32[]{:S(2)}, u32[]{:S(2)}) collective-permute-start(f32[2,3,10,130]{3,2,1,0:T(8,128)S(1)} %get-tuple-element.52), channel_id=1, source_target_pairs={{32,0},{64,32},{96,64},{128,96},{160,128},{192,160},{224,192},{256... | collective-permute-start | bytes 93608 | tf_op jit(solution)/shard_map/ppermute | solution.py:27
  150.4 6.9 %collective-permute-start.26 = (f32[2,16,3,130]{3,2,1,0:T(4,128)S(1)}, f32[2,16,3,130]{3,2,1,0:T(4,128)S(1)}, u32[]{:S(2)}, u32[]{:S(2)}) collective-permute-start(f32[2,16,3,130]{3,2,1,0:T(4,128)S(1)} %get-tuple-element.19), channel_id=1, source_target_pairs={{0,8},{8,16},{16,24},{1,9},{9,17},{17,25},{2,10},{10,18},{18,26},{... | collective-permute-start | bytes 149768 | tf_op jit(solution)/shard_map/ppermute | solution.py:25
  152.3 6.9 %collective-permute-start.27 = (f32[2,16,3,130]{3,2,1,0:T(4,128)S(1)}, f32[2,16,3,130]{3,2,1,0:T(4,128)S(1)}, u32[]{:S(2)}, u32[]{:S(2)}) collective-permute-start(f32[2,16,3,130]{3,2,1,0:T(4,128)S(1)} %get-tuple-element.20), channel_id=1, source_target_pairs={{8,0},{16,8},{24,16},{9,1},{17,9},{25,17},{10,2},{18,10},{26,18},{... | collective-permute-start | bytes 149768 | tf_op jit(solution)/shard_map/ppermute | solution.py:27
  159.5 8.5 %collective-permute-start.28 = (f32[2,16,16,3]{3,2,1,0:T(8,128)S(1)}, f32[2,16,16,3]{3,2,1,0:T(8,128)S(1)}, u32[]{:S(2)}, u32[]{:S(2)}) collective-permute-start(f32[2,16,16,3]{3,2,1,0:T(8,128)S(1)} %get-tuple-element.17), channel_id=1, source_target_pairs={{0,1},{1,2},{2,3},{3,4},{4,5},{5,6},{6,7},{8,9},{9,10},{10,11},{11... | collective-permute-start | bytes 18440 | tf_op jit(solution)/shard_map/ppermute | solution.py:25
  162.4 10.2 %collective-permute-start.29 = (f32[2,16,16,3]{3,2,1,0:T(8,128)S(1)}, f32[2,16,16,3]{3,2,1,0:T(8,128)S(1)}, u32[]{:S(2)}, u32[]{:S(2)}) collective-permute-start(f32[2,16,16,3]{3,2,1,0:T(8,128)S(1)} %get-tuple-element.18), channel_id=1, source_target_pairs={{1,0},{2,1},{3,2},{4,3},{5,4},{6,5},{7,6},{9,8},{10,9},{11,10},{12... | collective-permute-start | bytes 18440 | tf_op jit(solution)/shard_map/ppermute | solution.py:27
  175.2 0.8 copy-start
  (1 other events, 0.7 us)
where the time goes:
time: 238 us; the launch traced here: 237 us
  waiting for transfers between devices  81.2 us (34%)
  starting transfers between devices  75.3 us (32%)
  blocking collectives  58.3 us (24%)
  other arithmetic  13.6 us (6%)
  local copies, waits for them, and re-layouts  5.35 us (2%)
    psum x4, blocking collectives, over_axes(): x = lax.psum(x, axis)  58.3 us
    ppermute x15, waiting for transfers between devices, extended(): lax.ppermute(head, axis, [((i + 1) % count, i) for i in range(ends)])  53.7 us
    ppermute x15, starting transfers between devices, extended(): lax.ppermute(tail, axis, [(i, (i + 1) % count) for i in range(ends)])  41 us
    ppermute x15, starting transfers between devices, extended(): lax.ppermute(head, axis, [((i + 1) % count, i) for i in range(ends)])  34.3 us
    ppermute x15, waiting for transfers between devices, extended(): lax.ppermute(tail, axis, [(i, (i + 1) % count) for i in range(ends)])  27.6 us
  transfers between devices with their start and end apart: 30, of which 25 were waited for; matrix products, arithmetic and copies ran while one was open for 0% of the time, Pallas kernels for 0%

commit v1 on v0

v1 whole, which is shorter than its diff:
```python
import jax
import jax.numpy as jnp
from jax import lax
from jax.experimental import pallas as pl
from jax.experimental.pallas import tpu as pltpu
from jax.sharding import Mesh
from jax.sharding import PartitionSpec as P

STEPS = 4
GX = ("gx_0", "gx_1")
BX, BY, BZ = 8, 8, 128
SLAB = 2 * BX
HALO = 3 * STEPS + 1
STRIP = 16
TILES = 4
ROWS = TILES * BY
PAD = 8
PLANES = SLAB + 2 * HALO
NB = 10
SHORT = HALO - BX + 2
MSG = TILES * (NB + SHORT)
C0, C1, CS = 117.0, 15.0, 1.0 / 729.0

f32 = jnp.float32


def lanes():
    return lax.broadcasted_iota(jnp.int32, (8, 128), 1)


def pack_kernel(direction, residual, up, down):
    lane = lanes()
    for k, ref in enumerate((direction, residual)):
        high = jnp.zeros((8, 128), f32)
        low = jnp.zeros((8, 128), f32)
        for p in range(BX):
            here = (lane >= STRIP * p) & (lane < STRIP * (p + 1))
            v = ref[p]
            high = jnp.where(here, pltpu.roll(v, (STRIP * p - (BZ - STRIP)) % 128, 1), high)
            low = jnp.where(here, pltpu.roll(v, STRIP * p, 1) if p else v, low)
        up[k] = high
        down[k] = low


def powers_kernel(where_ref, own, low, high, mine, theirs, images, sums, *scratch):
    fields = scratch[:5]
    flat, g0_ref, g1_ref, g2_ref, x0_ref, x1_ref, x2_ref, zw, yw = scratch[5:]
    core, ix, iy, iz = where_ref[0], where_ref[1], where_ref[2], where_ref[3]
    lane = lanes()

    one = jnp.ones((8, 128), f32)
    has_l = jnp.where(iz > 0, 1.0, 0.0).astype(f32)
    has_r = where_ref[5].astype(f32)
    first, last = lane == 0, lane == 127
    inside = [one, jnp.where(lane < STRIP, has_r, jnp.where(lane >= 128 - STRIP, has_l, 0.0))]
    for k in range(2):
        if k == 0:
            m = one + jnp.where(first, has_l, 0.0) + jnp.where(last, has_r, 0.0)
            e_left = jnp.where(first, 2.0, 1.0)
            e_right = jnp.where(last, 2.0, 1.0)
            q = jnp.where(first, 2.0 * has_l, 1.0) + jnp.where(last, 2.0 * has_r, 1.0)
        else:
            m = jnp.where(first | last, 2.0, 1.0)
            e_left = jnp.where(first, 2.0, 1.0)
            e_right = jnp.where(last, 2.0, 1.0)
            q = e_left + e_right
        zw[k, 0] = C0 * m + q
        zw[k, 1] = C1 * m
        zw[k, 2] = m
        zw[k, 3] = e_left
        zw[k, 4] = e_right
        zw[k, 5] = inside[k] * CS
        zw[k, 6] = inside[k]

    row = lax.broadcasted_iota(jnp.int32, (ROWS, 128), 0)
    top, bottom = row % BY == 0, row % BY == BY - 1
    e_up = jnp.where(top, 2.0, 1.0)
    e_down = jnp.where(bottom, 2.0, 1.0)
    yw[0] = 1.0 + jnp.where(top & (row > 0), 1.0, 0.0) + jnp.where(bottom & (row < ROWS - 1), 1.0, 0.0)
    yw[1] = e_up
    yw[2] = e_down
    yw[3] = jnp.where(row > 0, e_up, 0.0) + jnp.where(row < ROWS - 1, e_down, 0.0)

    blank = jnp.zeros((PLANES, PAD, 128), f32)
    for ref in list(fields) + [g1_ref, g2_ref]:
        for k in range(2):
            ref[k, :, 0:PAD, :] = blank
            ref[k, :, PAD + ROWS : PAD + ROWS + PAD, :] = blank

    def place(x, t, center, left, right):
        p = x % BX
        rows = slice(PAD + BY * t, PAD + BY * (t + 1))
        fields[0][0, x + HALO, rows, :] = center
        shift_r = (-STRIP * p) % 128
        shift_l = (128 - STRIP - STRIP * p) % 128
        r = pltpu.roll(right, shift_r, 1) if shift_r else right
        l = pltpu.roll(left, shift_l, 1) if shift_l else left
        fields[0][1, x + HALO, rows, :] = jnp.where(
            lane < STRIP, r, jnp.where(lane >= 128 - STRIP, l, 0.0)
        )

    for t in range(TILES):
        for c in range(2):
            left, right = own[TILES * c + t, BX], own[TILES * c + t, BX + 1]
            for p in range(BX):
                place(BX * c + p, t, own[TILES * c + t, p], left, right)
        n = SHORT - 2
        base = SHORT * t
        for p in range(n):
            place(p - HALO, t, low[base + p], low[base + n], low[base + n + 1])
        base = SHORT * TILES + NB * t
        for p in range(BX):
            place(p - BX, t, low[base + p], low[base + BX], low[base + BX + 1])
        base = NB * t
        for p in range(BX):
            place(SLAB + p, t, high[base + p], high[base + BX], high[base + BX + 1])
        base = NB * TILES + SHORT * t
        for p in range(n):
            place(SLAB + BX + p, t, high[base + p], high[base + n], high[base + n + 1])

    lane_row = lax.broadcasted_iota(jnp.int32, (ROWS, 128), 1)

    def left_of(c, s, d):
        rc, rs = pltpu.roll(c, d, 1), pltpu.roll(s, d, 1)
        edge = lane_row < d
        return jnp.where(edge, rs, rc), jnp.where(edge, rc, rs)

    def right_of(c, s, d):
        rc, rs = pltpu.roll(c, 128 - d, 1), pltpu.roll(s, 128 - d, 1)
        edge = lane_row >= 128 - d
        return jnp.where(edge, rs, rc), jnp.where(edge, rc, rs)

    n_planes = where_ref[4]

    def in_grid(i):
        g = ix * SLAB + i - HALO
        return jnp.where((g >= 0) & (g < n_planes), 1.0, 0.0).astype(f32)

    def z_row(k, j):
        return zw[k, j][0:1, :]

    def around(ref, i):
        c, s = ref[0, i, PAD : PAD + ROWS, :], ref[1, i, PAD : PAD + ROWS, :]
        lc, ls = left_of(c, s, 1)
        rc, rs = right_of(c, s, 1)
        out = []
        for k, (v, a, b) in enumerate(((c, lc, rc), (s, ls, rs))):
            n = a + b
            n = n + (ref[k, i, PAD - 1 : PAD - 1 + ROWS, :] + ref[k, i, PAD + 1 : PAD + 1 + ROWS, :])
            n = n + (ref[k, i - 1, PAD : PAD + ROWS, :] + ref[k, i + 1, PAD : PAD + ROWS, :])
            out.append((v, n))
        return out

    for step in range(STEPS):
        source, target = fields[step], fields[step + 1]
        lo_b = 1 + 3 * step
        hi_b = PLANES - 1 - 3 * step

        def image_and_z(i, _, step=step, source=source):
            (c, nc), (s, ns) = around(source, i)
            if step == 0:
                center = jnp.where(core == 0, 6.0, 1.0).astype(f32)
                beside = jnp.where(core == 0, 1.0, 0.0).astype(f32)
                ac, as_ = center * c - beside * nc, center * s - beside * ns
            else:
                ac, as_ = 6.0 * c - nc, 6.0 * s - ns
            flat[step, i] = ac
            keep = in_grid(i)
            bc, bs = ac * (z_row(0, 5) * keep), as_ * (z_row(1, 5) * keep)
            l1c, l1s = left_of(bc, bs, 1)
            r1c, r1s = right_of(bc, bs, 1)
            l2c, l2s = left_of(bc, bs, 2)
            r2c, r2s = right_of(bc, bs, 2)
            for k, (b, l1, r1, l2, r2) in enumerate(((bc, l1c, r1c, l2c, r2c), (bs, l1s, r1s, l2s, r2s))):
                e = z_row(k, 3) * l1 + z_row(k, 4) * r1
                g0_ref[k, i] = z_row(k, 0) * b + C1 * e + (l2 + r2)
                g1_ref[k, i, PAD : PAD + ROWS, :] = z_row(k, 1) * b + (e + e)
                g2_ref[k, i, PAD : PAD + ROWS, :] = z_row(k, 2) * b
            return 0

        lax.fori_loop(lo_b, hi_b, image_and_z, 0)

        def along_y(i, _):
            for k in range(2):
                g1 = g1_ref[k, i, PAD : PAD + ROWS, :]
                g2 = g2_ref[k, i, PAD : PAD + ROWS, :]
                m, up, down, q = yw[0], yw[1], yw[2], yw[3]
                e1 = up * g1_ref[k, i, PAD - 1 : PAD - 1 + ROWS, :] + down * g1_ref[k, i, PAD + 1 : PAD + 1 + ROWS, :]
                e2 = up * g2_ref[k, i, PAD - 1 : PAD - 1 + ROWS, :] + down * g2_ref[k, i, PAD + 1 : PAD + 1 + ROWS, :]
                far = g2_ref[k, i, PAD - 2 : PAD - 2 + ROWS, :] + g2_ref[k, i, PAD + 2 : PAD + 2 + ROWS, :]
                x0_ref[k, i] = m * g0_ref[k, i] + e1 + (q * g2 + far)
                x1_ref[k, i] = m * g1 + (e2 + e2)
                x2_ref[k, i] = m * g2
            return 0

        lax.fori_loop(lo_b, hi_b, along_y, 0)

        def along_x(i, _, target=target):
            g = ix * SLAB + i - HALO
            keep = in_grid(i)
            p = g & (BX - 1)
            before = jnp.where(p == 0, 2.0, 1.0).astype(f32)
            after = jnp.where(p == BX - 1, 2.0, 1.0).astype(f32)
            some_before = jnp.where(g > 0, 1.0, 0.0).astype(f32)
            some_after = jnp.where(g < n_planes - 1, 1.0, 0.0).astype(f32)
            m = keep * (1.0 + (before - 1.0) * some_before + (after - 1.0) * some_after)
            q = keep * (before * some_before + after * some_after)
            wl, wr = keep * before, keep * after
            for k in range(2):
                v = m * x0_ref[k, i] + q * x2_ref[k, i]
                v = v + (wl * x1_ref[k, i - 1] + wr * x1_ref[k, i + 1])
                v = v + keep * (x2_ref[k, i - 2] + x2_ref[k, i + 2])
                if k == 1:
                    v = v * z_row(1, 6)
                target[k, i, PAD : PAD + ROWS, :] = v
            return 0

        lax.fori_loop(lo_b + 2, hi_b - 2, along_x, 0)

    def last_image(i, _):
        c, nc = around(fields[STEPS], i)[0]
        flat[STEPS, i] = 6.0 * c - nc
        return 0

    lax.fori_loop(HALO, HALO + SLAB, last_image, 0)

    rows = pl.ds(pl.multiple_of(PAD + BY * iy, 8), BY)
    flat_rows = pl.ds(pl.multiple_of(BY * iy, 8), BY)
    for j in range(1, STEPS + 1):
        mine[j - 1] = fields[j][0, pl.ds(HALO + BX * core, BX), rows, :]
        theirs[j - 1] = fields[j][0, pl.ds(HALO + BX * (1 - core), BX), rows, :]
    for j in range(STEPS + 1):
        images[j] = flat[j, pl.ds(HALO + BX * core, BX), flat_rows, :]
        theirs[STEPS + j] = flat[j, pl.ds(HALO + BX * (1 - core), BX), flat_rows, :]

    pairs = [(a, b) for a in range(STEPS + 1) for b in range(a, STEPS + 1)]
    totals = [jnp.zeros((8, 128), f32) for _ in pairs]
    for x in range(SLAB):
        fs = [fields[j][0, HALO + x, rows, :] for j in range(STEPS + 1)]
        im = [flat[j, HALO + x, flat_rows, :] for j in range(STEPS + 1)]
        totals = [total + fs[a] * im[b] for total, (a, b) in zip(totals, pairs)]
    sums[...] = jnp.zeros((16, 128), f32)
    for n, total in enumerate(totals):
        sums[n : n + 1, :] = jnp.sum(total, axis=0, keepdims=True)


def products_kernel(where_ref, mine, other, images, sums, direction, residual, powers, row, table):
    north = where_ref[0] == 0
    d, r = direction[...], residual[...]
    own = [jnp.where(north, d, r)] + [mine[j] for j in range(STEPS)]
    far = [jnp.where(north, r, d)] + [other[j] for j in range(STEPS)]
    p = [d] + [jnp.where(north, own[j], far[j]) for j in range(1, STEPS + 1)]
    z = [jnp.where(north, far[j], own[j]) for j in range(1, STEPS + 1)]
    for j in range(STEPS):
        powers[0, j] = p[j + 1]
        powers[1, j] = z[j]

    def fold(v):
        return jnp.sum(jnp.sum(v, axis=0), axis=0, keepdims=True)

    zero = jnp.zeros((1, 128), f32)
    local = {}
    n = 0
    for a in range(STEPS + 1):
        for b in range(a, STEPS + 1):
            local[a, b] = local[b, a] = sums[n : n + 1, :]
            n += 1
    image = [jnp.where(north, images[a], other[STEPS + a]) for a in range(STEPS + 1)]
    cross = [[fold(image[a] * z[b]) for b in range(STEPS)] for a in range(STEPS + 1)]
    table[...] = jnp.zeros((128, 128), f32)
    size = 2 * STEPS + 1
    for a in range(size):
        for b in range(size):
            if a <= STEPS and b <= STEPS:
                v = jnp.where(north, local[a, b], zero)
            elif a > STEPS and b > STEPS:
                v = jnp.where(north, zero, local[a - STEPS, b - STEPS])
            else:
                v = cross[min(a, b)][max(a, b) - STEPS - 1]
            table[size * a + b : size * a + b + 1, :] = v
    for a, v in enumerate(p + z):
        at = size * size + a
        table[at : at + 1, :] = fold(v * r)
    row[...] = lax.dot_general(
        jnp.ones((8, 128), f32),
        table[...],
        (((1,), (1,)), ((), ())),
        precision=lax.Precision.HIGHEST,
        preferred_element_type=f32,
    )[0:1, :]


def total_kernel(parts, gram, projections, *, scale):
    size = 2 * STEPS + 1
    total = parts[0]
    for n in range(1, parts.shape[0]):
        total = total + parts[n]
    total = total * scale
    wide = jnp.broadcast_to(total, (8, 128))
    for a in range(size):
        v = pltpu.roll(wide, (128 - size * a) % 128, 1) if a else wide
        gram[a : a + 1, :] = v[0:1, 0:size]
    v = pltpu.roll(wide, (128 - size * size) % 128, 1)
    projections[...] = v[0:1, 0:size]


VMEM = pl.BlockSpec(memory_space=pltpu.VMEM)
SMEM = pl.BlockSpec(memory_space=pltpu.SMEM)


def shaped(*dims):
    return jax.ShapeDtypeStruct(dims, f32)


def pack(direction, residual):
    return pl.pallas_call(
        pack_kernel,
        in_specs=[VMEM, VMEM],
        out_specs=[VMEM, VMEM],
        out_shape=[shaped(2, 8, 128), shaped(2, 8, 128)],
        name="pack",
    )(direction, residual)


def powers_of(where, own, low, high, interpret=False):
    padded = (2, PLANES, ROWS + 2 * PAD, 128)
    plain = (2, PLANES, ROWS, 128)
    return pl.pallas_call(
        powers_kernel,
        in_specs=[SMEM, VMEM, VMEM, VMEM],
        out_specs=[VMEM] * 4,
        out_shape=[
            shaped(STEPS, 8, 8, 128),
            shaped(2 * STEPS + 1, 8, 8, 128),
            shaped(STEPS + 1, 8, 8, 128),
            shaped(16, 128),
        ],
        scratch_shapes=[pltpu.VMEM(padded, f32)] * 5
        + [pltpu.VMEM((STEPS + 1, PLANES, ROWS, 128), f32)]
        + [pltpu.VMEM(plain, f32), pltpu.VMEM(padded, f32), pltpu.VMEM(padded, f32)]
        + [pltpu.VMEM(plain, f32)] * 3
        + [pltpu.VMEM((2, 7, 8, 128), f32), pltpu.VMEM((4, ROWS, 128), f32)],
        compiler_params=pltpu.CompilerParams(vmem_limit_bytes=48 * 1024 * 1024),
        interpret=interpret,
        name="powers",
    )(where, own, low, high)


def products(where, mine, other, images, sums, direction, residual, interpret=False):
    return pl.pallas_call(
        products_kernel,
        in_specs=[SMEM] + [VMEM] * 6,
        out_specs=[VMEM, VMEM],
        out_shape=[shaped(2, STEPS, 8, 8, 128), shaped(1, 128)],
        scratch_shapes=[pltpu.VMEM((128, 128), f32)],
        interpret=interpret,
        name="products",
    )(where, mine, other, images, sums, direction, residual)


def totals(parts, scale, interpret=False):
    size = 2 * STEPS + 1

    def kernel(parts_ref, gram, projections):
        total_kernel(parts_ref, gram, projections, scale=scale)

    return pl.pallas_call(
        kernel,
        in_specs=[VMEM],
        out_specs=[VMEM, VMEM],
        out_shape=[shaped(size, size), shaped(1, size)],
        interpret=interpret,
        name="totals",
    )(parts)


def block_message(cells, left, right):
    return jnp.concatenate([cells, left[None], right[None]], axis=0)


def x_messages(own):
    n = SHORT - 2
    first, second = own[:TILES], own[TILES:]
    flat = lambda v: v.reshape(-1, 8, 128)
    up = jnp.concatenate([flat(first[:, BX - n :]), flat(second)], axis=0)
    short = jnp.concatenate([second[:, :n], second[:, BX:]], axis=1)
    down = jnp.concatenate([flat(first), flat(short)], axis=0)
    return up, down


def forward(n):
    return [(i, i + 1) for i in range(n - 1)]


def backward(n):
    return [(i + 1, i) for i in range(n - 1)]


def everyone(x, axes, count):
    return lax.all_to_all(jnp.broadcast_to(x[None], (count,) + x.shape), axes, 0, 0)


def local(residual, direction):
    nx, ny, nz = lax.axis_size("gx_0"), lax.axis_size("gy"), lax.axis_size("gz")
    iz = lax.axis_index("gz")
    where = jnp.stack(
        [
            lax.axis_index("gx_1"),
            lax.axis_index("gx_0"),
            lax.axis_index("gy"),
            iz,
            jnp.int32(nx * SLAB),
            jnp.where(iz < nz - 1, 1, 0),
        ]
    ).astype(jnp.int32)
    up, down = pack(direction, residual)
    left = lax.ppermute(up, "gz", forward(nz))
    right = lax.ppermute(down, "gz", backward(nz))
    message = jnp.stack(
        [block_message(direction, left[0], right[0]), block_message(residual, left[1], right[1])]
    )
    message = jnp.broadcast_to(message[:, None], (2, TILES) + message.shape[1:])
    own = lax.all_to_all(message.reshape((2 * TILES,) + message.shape[2:]), ("gx_1", "gy"), 0, 0)
    send_up, send_down = x_messages(own)
    low = lax.ppermute(send_up, "gx_0", forward(nx))
    high = lax.ppermute(send_down, "gx_0", backward(nx))
    mine, theirs, images, sums = powers_of(where, own, low, high)
    other = lax.ppermute(theirs, "gx_1", [(0, 1), (1, 0)])
    powers, row = products(where, mine, other, images, sums, direction, residual)
    row = jnp.sum(everyone(row, ("gy", "gz"), ny * nz), axis=0)
    parts = everyone(row, GX, 2 * nx)
    cells = float(2 * nx * BX * ny * BY * nz * BZ)
    gram, projections = totals(parts, 1.0 / cells)
    return powers, gram, projections.reshape(-1)


def solution(mesh):
    torus = Mesh(
        mesh.devices.reshape(mesh.shape["gx"] // 2, 2, mesh.shape["gy"], mesh.shape["gz"]),
        ("gx_0", "gx_1", "gy", "gz"),
    )
    return jax.shard_map(
        local,
        mesh=torus,
        in_specs=(P(GX, "gy", "gz"), P(GX, "gy", "gz")),
        out_specs=(P(None, None, GX, "gy", "gz"), P(), P()),
        check_vma=False,
    )
```

time: 238 us -> 126 us (0.53)
  the two profiles are of different devices: /device:TPU:2 before, /device:TPU:1 now
where the time goes in v1:
time: 126 us
  blocking collectives  59.6 us (47%)
  Pallas kernels  37.6 us (30%)
  waiting for transfers between devices  12.8 us (10%)
  starting transfers between devices  11.2 us (9%)
  local copies, waits for them, and re-layouts  3.47 us (3%)
    all_to_all x2, blocking collectives, everyone(): lax.all_to_all(jnp.broadcast_to(x[None], (count,) + x.shape), axes, 0, 0)  40.8 us
    pallas_call x1, Pallas kernels, powers_of(): pl.pallas_call(powers_kernel, in_specs=[SMEM, VMEM, VMEM, VMEM], out_spec...  32.7 us
    all_to_all x1, blocking collectives, local(): lax.all_to_all(message.reshape((2 * TILES,) + message.shape[2:]), ('gx_1'...  18.8 us
    ppermute x1, waiting for transfers between devices, local(): low = lax.ppermute(send_up, 'gx_0', forward(nx))  4.39 us
    ppermute x1, starting transfers between devices, local(): left = lax.ppermute(up, 'gz', forward(nz))  4.14 us
    ppermute x1, waiting for transfers between devices, local(): high = lax.ppermute(send_down, 'gx_0', backward(nx))  3.92 us
    unnamed x16, local copies, waits for them, and re-layouts  3.3 us
    ppermute x1, waiting for transfers between devices, local(): right = lax.ppermute(down, 'gz', backward(nz))  3.28 us
  transfers between devices with their start and end apart: 5, of which 4 were waited for; matrix products, arithmetic and copies ran while one was open for 0% of the time, Pallas kernels for 0%

profile of v1, /device:TPU:1, one launch (start us, length us, event | category | flops | bytes accessed | tf_op | source)
XLA Modules:
  0.0 125.5 jit_solution(2122018057113463149)
XLA Ops:
  0.6 0.0 copy-start.5
  0.6 1.5 %pack.1 = (f32[2,8,128]{2,1,0:T(8,128)}, f32[2,8,128]{2,1,0:T(8,128)}) custom-call(f32[8,8,128]{2,1,0:T(8,128)} %direction.3, f32[8,8,128]{2,1,0:T(8,128)} %residual.3), custom_call_target="tpu_custom_call" | custom-call | tf_op jit(solution)/shard_map/pack/pallas_call | solution.py:316
  2.2 0.0 copy-start.4
  2.2 4.1 %collective-permute-start = (f32[2,8,128]{2,1,0:T(8,128)}, f32[2,8,128]{2,1,0:T(8,128)S(1)}, u32[]{:S(2)}, u32[]{:S(2)}) collective-permute-start(f32[2,8,128]{2,1,0:T(8,128)} %get-tuple-element.13), channel_id=1, source_target_pairs={{0,1},{1,2},{2,3},{3,4},{4,5},{5,6},{6,7},{8,9},{9,10},{10,11},{11... | collective-permute-start | bytes 24584 | tf_op jit(solution)/shard_map/ppermute | solution.py:417
  6.3 1.3 %collective-permute-start.1 = (f32[2,8,128]{2,1,0:T(8,128)}, f32[2,8,128]{2,1,0:T(8,128)S(1)}, u32[]{:S(2)}, u32[]{:S(2)}) collective-permute-start(f32[2,8,128]{2,1,0:T(8,128)} %get-tuple-element.14), channel_id=1, source_target_pairs={{1,0},{2,1},{3,2},{4,3},{5,4},{6,5},{7,6},{9,8},{10,9},{11,10},{12... | collective-permute-start | bytes 24584 | tf_op jit(solution)/shard_map/ppermute | solution.py:418
  7.6 0.0 collective-permute-done
  7.6 3.3 %collective-permute-done.1 = f32[2,8,128]{2,1,0:T(8,128)S(1)} collective-permute-done((f32[2,8,128]{2,1,0:T(8,128)}, f32[2,8,128]{2,1,0:T(8,128)S(1)}, u32[]{:S(2)}, u32[]{:S(2)}) %collective-permute-start.1) | collective-permute-done | bytes 8224 | tf_op jit(solution)/shard_map/ppermute | solution.py:418
  10.9 0.0 copy-done.5
  10.9 0.0 copy-done.4
  11.0 18.8 %all_to_all.15.own = f32[8,10,8,128]{3,2,1,0:T(8,128)S(1)} all-to-all(f32[8,10,8,128]{3,2,1,0:T(8,128)S(1)} %bitcast.17), channel_id=1, replica_groups=mesh['gx_0'=12,'gx_1'=2,'gy'=4,'gz'=8] {'gx_1','gy'}, dimensions={0} | all-to-all | bytes 655360 | tf_op jit(solution)/shard_map/all_to_all | solution.py:423
  29.9 1.3 %collective-permute-start.2 = (f32[68,8,128]{2,1,0:T(8,128)S(1)}, f32[68,8,128]{2,1,0:T(8,128)S(1)}, u32[]{:S(2)}, u32[]{:S(2)}) collective-permute-start(f32[68,8,128]{2,1,0:T(8,128)S(1)} %pad_maximum_fusion), channel_id=1, source_target_pairs={{0,64},{64,128},{128,192},{192,256},{256,320},{320,384},{384,448},... | collective-permute-start | bytes 835592 | tf_op jit(solution)/shard_map/ppermute | solution.py:425
  31.3 1.3 %collective-permute-start.3 = (f32[68,8,128]{2,1,0:T(8,128)S(1)}, f32[68,8,128]{2,1,0:T(8,128)S(1)}, u32[]{:S(2)}, u32[]{:S(2)}) collective-permute-start(f32[68,8,128]{2,1,0:T(8,128)S(1)} %pad_maximum_fusion.1), channel_id=1, source_target_pairs={{64,0},{128,64},{192,128},{256,192},{320,256},{384,320},{448,384},... | collective-permute-start | bytes 835592 | tf_op jit(solution)/shard_map/ppermute | solution.py:426
  32.6 0.1 stack.32.where_ref
  32.7 0.0 copy-start.3
  32.7 4.4 %collective-permute-done.2.low = f32[68,8,128]{2,1,0:T(8,128)S(1)} collective-permute-done((f32[68,8,128]{2,1,0:T(8,128)S(1)}, f32[68,8,128]{2,1,0:T(8,128)S(1)}, u32[]{:S(2)}, u32[]{:S(2)}) %collective-permute-start.2) | collective-permute-done | bytes 278560 | tf_op jit(solution)/shard_map/ppermute | solution.py:425
  37.1 3.9 %collective-permute-done.3.high = f32[68,8,128]{2,1,0:T(8,128)S(1)} collective-permute-done((f32[68,8,128]{2,1,0:T(8,128)S(1)}, f32[68,8,128]{2,1,0:T(8,128)S(1)}, u32[]{:S(2)}, u32[]{:S(2)}) %collective-permute-start.3) | collective-permute-done | bytes 278560 | tf_op jit(solution)/shard_map/ppermute | solution.py:426
  41.0 32.7 %powers.1 = (f32[4,8,8,128]{3,2,1,0:T(8,128)S(1)}, f32[9,8,8,128]{3,2,1,0:T(8,128)S(1)}, f32[5,8,8,128]{3,2,1,0:T(8,128)S(1)}, f32[16,128]{1,0:T(8,128)S(1)}) custom-call(s32[6]{0:T(128)S(1)} %stack.32.where_ref, f32[8,10,8,128]{3,2,1,0:T(8,128)S(1)} %all_to_all.15.own, f32[68,8,128]{2,1,0:T(8,128)S(1)} %collective-permute-done.2.low, ...), custom_call_target="tpu_custom_call" | custom-call | tf_op jit(solution)/shard_map/powers/pallas_call | solution.py:328
  73.7 0.0 copy-done.3
  73.7 0.0 copy-start
  73.7 0.7 copy-done
  74.3 0.0 copy-start.1
  74.3 0.6 copy-done.1
  75.0 0.0 copy-start.2
  75.0 0.6 copy-done.2
  75.6 3.1 %collective-permute-start.4 = (f32[9,8,8,128]{3,2,1,0:T(8,128)S(1)}, f32[9,8,8,128]{3,2,1,0:T(8,128)S(1)}, u32[]{:S(2)}, u32[]{:S(2)}) collective-permute-start(f32[9,8,8,128]{3,2,1,0:T(8,128)S(1)} %get-tuple-element.16), channel_id=1, source_target_pairs={{0,32},{32,0},{1,33},{33,1},{2,34},{34,2},{3,35},{35,3},{4,36},{36... | collective-permute-start | bytes 884744 | tf_op jit(solution)/shard_map/ppermute | solution.py:428
  78.7 1.2 collective-permute-done.4.other
  79.9 0.7 copy-done.6
  80.6 2.0 %products.1 = (f32[2,4,8,8,128]{4,3,2,1,0:T(8,128)}, f32[1,128]{1,0:T(1,128)}) custom-call(s32[6]{0:T(128)} %copy-done.3, f32[4,8,8,128]{3,2,1,0:T(8,128)} %copy-done.1, f32[9,8,8,128]{3,2,1,0:T(8,128)} %copy-done.6, f32[5,8,8,128]{3,2,1,0:T(8,128)} %copy-done, f32[16,128]{1,0:T(8,128)} %copy-done.2, f32[8,8,128]{2,1,0:T(8,128)} %direction.3, ...), custom_call_target="tpu_custom_call" | custom-call | tf_op jit(solution)/shard_map/products/pallas_call | solution.py:350
  82.7 0.7 copy-done.7
  83.3 14.7 %all_to_all.16 = f32[32,1,128]{2,1,0:T(1,128)S(1)} all-to-all(f32[32,1,128]{2,1,0:T(1,128)S(1)} %broadcast_in_dim.10), channel_id=1, replica_groups=mesh['gx_0'=12,'gx_1'=2,'gy'=4,'gz'=8] {'gy','gz'}, dimensions={0} | all-to-all | bytes 32768 | tf_op jit(solution)/shard_map/all_to_all | solution.py:400
  98.1 26.0 %all_to_all.17.parts_ref = f32[24,1,128]{2,1,0:T(1,128)} all-to-all(f32[24,1,128]{2,1,0:T(1,128)S(1)} %broadcast_in_dim.11), channel_id=1, replica_groups=mesh['gx_0'=12,'gx_1'=2,'gy'=4,'gz'=8] {'gx_0','gx_1'}, dimensions={0} | all-to-all | bytes 24576 | tf_op jit(solution)/shard_map/all_to_all | solution.py:400
  124.1 1.4 %totals.1 = (f32[9,9]{1,0:T(8,128)}, f32[1,9]{1,0:T(1,128)}) custom-call(f32[24,1,128]{2,1,0:T(1,128)} %all_to_all.17.parts_ref), custom_call_target="tpu_custom_call" | custom-call | tf_op jit(solution)/shard_map/totals/pallas_call | solution.py:367
  (17 shorter events, 0.2 us)
Async XLA Ops:
  0.6 10.3 %copy-start.5 = (f32[8,8,128]{2,1,0:T(8,128)S(1)}, f32[8,8,128]{2,1,0:T(8,128)}, u32[]{:S(2)}) copy-start(f32[8,8,128]{2,1,0:T(8,128)} %residual.3) | copy-start | bytes 98308
  2.2 8.8 %copy-start.4 = (f32[8,8,128]{2,1,0:T(8,128)S(1)}, f32[8,8,128]{2,1,0:T(8,128)}, u32[]{:S(2)}) copy-start(f32[8,8,128]{2,1,0:T(8,128)} %direction.3) | copy-start | bytes 98308
  2.2 5.4 %collective-permute-start = (f32[2,8,128]{2,1,0:T(8,128)}, f32[2,8,128]{2,1,0:T(8,128)S(1)}, u32[]{:S(2)}, u32[]{:S(2)}) collective-permute-start(f32[2,8,128]{2,1,0:T(8,128)} %get-tuple-element.13), channel_id=1, source_target_pairs={{0,1},{1,2},{2,3},{3,4},{4,5},{5,6},{6,7},{8,9},{9,10},{10,11},{11... | collective-permute-start | bytes 24584 | tf_op jit(solution)/shard_map/ppermute | solution.py:417
  6.3 4.6 %collective-permute-start.1 = (f32[2,8,128]{2,1,0:T(8,128)}, f32[2,8,128]{2,1,0:T(8,128)S(1)}, u32[]{:S(2)}, u32[]{:S(2)}) collective-permute-start(f32[2,8,128]{2,1,0:T(8,128)} %get-tuple-element.14), channel_id=1, source_target_pairs={{1,0},{2,1},{3,2},{4,3},{5,4},{6,5},{7,6},{9,8},{10,9},{11,10},{12... | collective-permute-start | bytes 24584 | tf_op jit(solution)/shard_map/ppermute | solution.py:418
  29.9 7.2 %collective-permute-start.2 = (f32[68,8,128]{2,1,0:T(8,128)S(1)}, f32[68,8,128]{2,1,0:T(8,128)S(1)}, u32[]{:S(2)}, u32[]{:S(2)}) collective-permute-start(f32[68,8,128]{2,1,0:T(8,128)S(1)} %pad_maximum_fusion), channel_id=1, source_target_pairs={{0,64},{64,128},{128,192},{192,256},{256,320},{320,384},{384,448},... | collective-permute-start | bytes 835592 | tf_op jit(solution)/shard_map/ppermute | solution.py:425
  31.3 9.7 %collective-permute-start.3 = (f32[68,8,128]{2,1,0:T(8,128)S(1)}, f32[68,8,128]{2,1,0:T(8,128)S(1)}, u32[]{:S(2)}, u32[]{:S(2)}) collective-permute-start(f32[68,8,128]{2,1,0:T(8,128)S(1)} %pad_maximum_fusion.1), channel_id=1, source_target_pairs={{64,0},{128,64},{192,128},{256,192},{320,256},{384,320},{448,384},... | collective-permute-start | bytes 835592 | tf_op jit(solution)/shard_map/ppermute | solution.py:426
  32.7 41.0 %copy-start.3 = (s32[6]{0:T(128)}, s32[6]{0:T(128)S(1)}, u32[]{:S(2)}) copy-start(s32[6]{0:T(128)S(1)} %stack.32.where_ref) | copy-start | bytes 76
  73.7 0.7 copy-start
  74.3 0.6 copy-start.1
  75.0 0.6 copy-start.2
  75.6 4.3 %collective-permute-start.4 = (f32[9,8,8,128]{3,2,1,0:T(8,128)S(1)}, f32[9,8,8,128]{3,2,1,0:T(8,128)S(1)}, u32[]{:S(2)}, u32[]{:S(2)}) collective-permute-start(f32[9,8,8,128]{3,2,1,0:T(8,128)S(1)} %get-tuple-element.16), channel_id=1, source_target_pairs={{0,32},{32,0},{1,33},{33,1},{2,34},{34,2},{3,35},{35,3},{4,36},{36... | collective-permute-start | bytes 884744 | tf_op jit(solution)/shard_map/ppermute | solution.py:428
  79.9 0.7 copy-start.6
  82.7 0.7 copy-start.7

commit v2 on v1

--- a/solution.py
+++ b/solution.py
@@ -19,6 +19,9 @@
 NB = 10
 SHORT = HALO - BX + 2
 MSG = TILES * (NB + SHORT)
+UNROLL = 4
+LEAD = UNROLL + 6
+ORIGIN = LEAD + HALO
 C0, C1, CS = 117.0, 15.0, 1.0 / 729.0
 
 f32 = jnp.float32
@@ -44,7 +47,7 @@
 
 def powers_kernel(where_ref, own, low, high, mine, theirs, images, sums, *scratch):
     fields = scratch[:5]
-    flat, g0_ref, g1_ref, g2_ref, x0_ref, x1_ref, x2_ref, zw, yw = scratch[5:]
+    flat, b_ref, g0_ref, g1_ref, g2_ref, x0_ref, x1_ref, x2_ref, zw, yw = scratch[5:]
     core, ix, iy, iz = where_ref[0], where_ref[1], where_ref[2], where_ref[3]
     lane = lanes()
 
@@ -81,21 +84,26 @@
     yw[2] = e_down
     yw[3] = jnp.where(row > 0, e_up, 0.0) + jnp.where(row < ROWS - 1, e_down, 0.0)
 
-    blank = jnp.zeros((PLANES, PAD, 128), f32)
-    for ref in list(fields) + [g1_ref, g2_ref]:
-        for k in range(2):
-            ref[k, :, 0:PAD, :] = blank
-            ref[k, :, PAD + ROWS : PAD + ROWS + PAD, :] = blank
+    blank = jnp.zeros((PAD, 128), f32)
+
+    def clear(i, _):
+        for ref in list(fields) + [g1_ref, g2_ref]:
+            for k in range(2):
+                ref[k, i, 0:PAD, :] = blank
+                ref[k, i, PAD + ROWS : PAD + ROWS + PAD, :] = blank
+        return 0
+
+    lax.fori_loop(LEAD, LEAD + PLANES, clear, 0)
 
     def place(x, t, center, left, right):
         p = x % BX
         rows = slice(PAD + BY * t, PAD + BY * (t + 1))
-        fields[0][0, x + HALO, rows, :] = center
+        fields[0][0, x + ORIGIN, rows, :] = center
         shift_r = (-STRIP * p) % 128
         shift_l = (128 - STRIP - STRIP * p) % 128
         r = pltpu.roll(right, shift_r, 1) if shift_r else right
         l = pltpu.roll(left, shift_l, 1) if shift_l else left
-        fields[0][1, x + HALO, rows, :] = jnp.where(
+        fields[0][1, x + ORIGIN, rows, :] = jnp.where(
             lane < STRIP, r, jnp.where(lane >= 128 - STRIP, l, 0.0)
         )
 
@@ -133,7 +141,7 @@
     n_planes = where_ref[4]
 
     def in_grid(i):
-        g = ix * SLAB + i - HALO
+        g = ix * SLAB + i - ORIGIN
         return jnp.where((g >= 0) & (g < n_planes), 1.0, 0.0).astype(f32)
 
     def z_row(k, j):
@@ -153,10 +161,10 @@
 
     for step in range(STEPS):
         source, target = fields[step], fields[step + 1]
-        lo_b = 1 + 3 * step
-        hi_b = PLANES - 1 - 3 * step
-
-        def image_and_z(i, _, step=step, source=source):
+        lo_b = LEAD + 1 + 3 * step
+        hi_b = LEAD + PLANES - 1 - 3 * step
+
+        def image(i, step=step, source=source):
             (c, nc), (s, ns) = around(source, i)
             if step == 0:
                 center = jnp.where(core == 0, 6.0, 1.0).astype(f32)
@@ -166,7 +174,11 @@
                 ac, as_ = 6.0 * c - nc, 6.0 * s - ns
             flat[step, i] = ac
             keep = in_grid(i)
-            bc, bs = ac * (z_row(0, 5) * keep), as_ * (z_row(1, 5) * keep)
+            b_ref[0, i] = ac * (z_row(0, 5) * keep)
+            b_ref[1, i] = as_ * (z_row(1, 5) * keep)
+
+        def along_z(i):
+            bc, bs = b_ref[0, i], b_ref[1, i]
             l1c, l1s = left_of(bc, bs, 1)
             r1c, r1s = right_of(bc, bs, 1)
             l2c, l2s = left_of(bc, bs, 2)
@@ -176,11 +188,9 @@
                 g0_ref[k, i] = z_row(k, 0) * b + C1 * e + (l2 + r2)
                 g1_ref[k, i, PAD : PAD + ROWS, :] = z_row(k, 1) * b + (e + e)
                 g2_ref[k, i, PAD : PAD + ROWS, :] = z_row(k, 2) * b
-            return 0
-
-        lax.fori_loop(lo_b, hi_b, image_and_z, 0)
-
-        def along_y(i, _):
+
+
+        def along_y(i):
             for k in range(2):
                 g1 = g1_ref[k, i, PAD : PAD + ROWS, :]
                 g2 = g2_ref[k, i, PAD : PAD + ROWS, :]
@@ -191,12 +201,10 @@
                 x0_ref[k, i] = m * g0_ref[k, i] + e1 + (q * g2 + far)
                 x1_ref[k, i] = m * g1 + (e2 + e2)
                 x2_ref[k, i] = m * g2
-            return 0
-
-        lax.fori_loop(lo_b, hi_b, along_y, 0)
-
-        def along_x(i, _, target=target):
-            g = ix * SLAB + i - HALO
+
+
+        def along_x(i, target=target):
+            g = ix * SLAB + i - ORIGIN
             keep = in_grid(i)
             p = g & (BX - 1)
             before = jnp.where(p == 0, 2.0, 1.0).astype(f32)
@@ -213,31 +221,46 @@
                 if k == 1:
                     v = v * z_row(1, 6)
                 target[k, i, PAD : PAD + ROWS, :] = v
+
+        def turn(n, _, lo_b=lo_b):
+            i = lo_b + UNROLL * n
+            for u in range(UNROLL):
+                along_z(i + u - UNROLL)
+            for u in range(UNROLL):
+                along_y(i + u - UNROLL)
+            for u in range(UNROLL):
+                along_x(i + u - UNROLL - 2)
+            for u in range(UNROLL):
+                image(i + u)
             return 0
 
-        lax.fori_loop(lo_b + 2, hi_b - 2, along_x, 0)
-
-    def last_image(i, _):
+        lax.fori_loop(0, -(-(hi_b - lo_b) // UNROLL) + 1, turn, 0)
+
+    def last_image(i):
         c, nc = around(fields[STEPS], i)[0]
         flat[STEPS, i] = 6.0 * c - nc
+
+    def last_turn(n, _):
+        for u in range(SLAB // 2):
+            last_image(ORIGIN + SLAB // 2 * n + u)
         return 0
 
-    lax.fori_loop(HALO, HALO + SLAB, last_image, 0)
+    lax.fori_loop(0, 2, last_turn, 0)
 
     rows = pl.ds(pl.multiple_of(PAD + BY * iy, 8), BY)
     flat_rows = pl.ds(pl.multiple_of(BY * iy, 8), BY)
     for j in range(1, STEPS + 1):
-        mine[j - 1] = fields[j][0, pl.ds(HALO + BX * core, BX), rows, :]
-        theirs[j - 1] = fields[j][0, pl.ds(HALO + BX * (1 - core), BX), rows, :]
+        mine[j - 1] = fields[j][0, pl.ds(ORIGIN + BX * core, BX), rows, :]
+        theirs[j - 1] = fields[j][0, pl.ds(ORIGIN + BX * (1 - core), BX), rows, :]
     for j in range(STEPS + 1):
-        images[j] = flat[j, pl.ds(HALO + BX * core, BX), flat_rows, :]
-        theirs[STEPS + j] = flat[j, pl.ds(HALO + BX * (1 - core), BX), flat_rows, :]
+        images[j] = flat[j, pl.ds(ORIGIN + BX * core, BX), flat_rows, :]
+        theirs[STEPS + j] = flat[j, pl.ds(ORIGIN + BX * (1 - core), BX), flat_rows, :]
 
     pairs = [(a, b) for a in range(STEPS + 1) for b in range(a, STEPS + 1)]
     totals = [jnp.zeros((8, 128), f32) for _ in pairs]
     for x in range(SLAB):
-        fs = [fields[j][0, HALO + x, rows, :] for j in range(STEPS + 1)]
-        im = [flat[j, HALO + x, flat_rows, :] for j in range(STEPS + 1)]
+        fs = [fields[j][0, ORIGIN + x, rows, :] for j in range(STEPS + 1)]
+        im = [flat[j, ORIGIN + x, flat_rows, :] for j in range(STEPS + 1)]
         totals = [total + fs[a] * im[b] for total, (a, b) in zip(totals, pairs)]
     sums[...] = jnp.zeros((16, 128), f32)
     for n, total in enumerate(totals):
@@ -318,13 +341,14 @@
         in_specs=[VMEM, VMEM],
         out_specs=[VMEM, VMEM],
         out_shape=[shaped(2, 8, 128), shaped(2, 8, 128)],
+        compiler_params=pltpu.CompilerParams(vmem_limit_bytes=2 * 1024 * 1024),
         name="pack",
     )(direction, residual)
 
 
 def powers_of(where, own, low, high, interpret=False):
-    padded = (2, PLANES, ROWS + 2 * PAD, 128)
-    plain = (2, PLANES, ROWS, 128)
+    padded = (2, PLANES + 2 * LEAD, ROWS + 2 * PAD, 128)
+    plain = (2, PLANES + 2 * LEAD, ROWS, 128)
     return pl.pallas_call(
         powers_kernel,
         in_specs=[SMEM, VMEM, VMEM, VMEM],
@@ -336,11 +360,11 @@
             shaped(16, 128),
         ],
         scratch_shapes=[pltpu.VMEM(padded, f32)] * 5
-        + [pltpu.VMEM((STEPS + 1, PLANES, ROWS, 128), f32)]
-        + [pltpu.VMEM(plain, f32), pltpu.VMEM(padded, f32), pltpu.VMEM(padded, f32)]
+        + [pltpu.VMEM((STEPS + 1, PLANES + 2 * LEAD, ROWS, 128), f32)]
+        + [pltpu.VMEM(plain, f32), pltpu.VMEM(plain, f32), pltpu.VMEM(padded, f32), pltpu.VMEM(padded, f32)]
         + [pltpu.VMEM(plain, f32)] * 3
         + [pltpu.VMEM((2, 7, 8, 128), f32), pltpu.VMEM((4, ROWS, 128), f32)],
-        compiler_params=pltpu.CompilerParams(vmem_limit_bytes=48 * 1024 * 1024),
+        compiler_params=pltpu.CompilerParams(vmem_limit_bytes=44 * 1024 * 1024),
         interpret=interpret,
         name="powers",
     )(where, own, low, high)
@@ -354,6 +378,7 @@
         out_shape=[shaped(2, STEPS, 8, 8, 128), shaped(1, 128)],
         scratch_shapes=[pltpu.VMEM((128, 128), f32)],
         interpret=interpret,
+        compiler_params=pltpu.CompilerParams(vmem_limit_bytes=2 * 1024 * 1024),
         name="products",
     )(where, mine, other, images, sums, direction, residual)
 
@@ -370,6 +395,7 @@
         out_specs=[VMEM, VMEM],
         out_shape=[shaped(size, size), shaped(1, size)],
         interpret=interpret,
+        compiler_params=pltpu.CompilerParams(vmem_limit_bytes=2 * 1024 * 1024),
         name="totals",
     )(parts)
 

time: 126 us -> 102 us (0.81)
  Pallas kernels: 37.6 us -> 15.6 us
  local copies, waits for them, and re-layouts: 3.47 us -> 1.7 us
    pallas_call x1, Pallas kernels: 32.7 us -> 13.4 us  [powers_of(): pl.pallas_call(powers_kernel, in_specs=[SMEM, VMEM, VMEM, VMEM], out_spec...]
    unnamed x16 -> x8, local copies, waits for them, and re-layouts: 3.3 us -> 1.52 us
    pallas_call x1, Pallas kernels: 1.52 us -> 0.09 us  [pack(): pl.pallas_call(pack_kernel, in_specs=[VMEM, VMEM], out_specs=[VMEM, VMEM]...]
where the time goes in v2:
time: 102 us; the launch traced here: 101 us
  blocking collectives  59.5 us (58%)
  Pallas kernels  15.6 us (15%)
  waiting for transfers between devices  12.6 us (12%)
  starting transfers between devices  11.1 us (11%)
  local copies, waits for them, and re-layouts  1.7 us (2%)
    all_to_all x2, blocking collectives, everyone(): lax.all_to_all(jnp.broadcast_to(x[None], (count,) + x.shape), axes, 0, 0)  40.6 us
    all_to_all x1, blocking collectives, local(): lax.all_to_all(message.reshape((2 * TILES,) + message.shape[2:]), ('gx_1'...  18.8 us
    pallas_call x1, Pallas kernels, powers_of(): pl.pallas_call(powers_kernel, in_specs=[SMEM, VMEM, VMEM, VMEM], out_spec...  13.4 us
    ppermute x1, waiting for transfers between devices, local(): low = lax.ppermute(send_up, 'gx_0', forward(nx))  4.39 us
    ppermute x1, starting transfers between devices, local(): left = lax.ppermute(up, 'gz', forward(nz))  4.02 us
    ppermute x1, waiting for transfers between devices, local(): high = lax.ppermute(send_down, 'gx_0', backward(nx))  3.92 us
    ppermute x1, starting transfers between devices, local(): other = lax.ppermute(theirs, 'gx_1', [(0, 1), (1, 0)])  3.16 us
    ppermute x1, waiting for transfers between devices, local(): right = lax.ppermute(down, 'gz', backward(nz))  3.07 us
  transfers between devices with their start and end apart: 5, of which 4 were waited for; matrix products, arithmetic and copies ran while one was open for 0% of the time, Pallas kernels for 0%

profile of v2, /device:TPU:1, one launch (start us, length us, event | category | flops | bytes accessed | tf_op | source)
XLA Modules:
  0.0 101.3 jit_solution(1132635502227643999)
XLA Ops:
  0.6 0.0 copy-start
  0.6 0.7 copy-done
  1.4 0.0 copy-start.2
  1.4 0.8 copy-done.2
  2.1 0.0 copy-start.3
  2.2 0.1 pack.1
  2.2 0.0 copy-start.1
  2.3 4.0 %collective-permute-start = (f32[2,8,128]{2,1,0:T(8,128)S(1)}, f32[2,8,128]{2,1,0:T(8,128)S(1)}, u32[]{:S(2)}, u32[]{:S(2)}) collective-permute-start(f32[2,8,128]{2,1,0:T(8,128)S(1)} %get-tuple-element.13), channel_id=1, source_target_pairs={{0,1},{1,2},{2,3},{3,4},{4,5},{5,6},{6,7},{8,9},{9,10},{10,11},{11... | collective-permute-start | bytes 24584 | tf_op jit(solution)/shard_map/ppermute | solution.py:443
  6.3 1.3 %collective-permute-start.1 = (f32[2,8,128]{2,1,0:T(8,128)S(1)}, f32[2,8,128]{2,1,0:T(8,128)S(1)}, u32[]{:S(2)}, u32[]{:S(2)}) collective-permute-start(f32[2,8,128]{2,1,0:T(8,128)S(1)} %get-tuple-element.14), channel_id=1, source_target_pairs={{1,0},{2,1},{3,2},{4,3},{5,4},{6,5},{7,6},{9,8},{10,9},{11,10},{12... | collective-permute-start | bytes 24584 | tf_op jit(solution)/shard_map/ppermute | solution.py:444
  7.6 0.0 collective-permute-done
  7.6 3.1 %collective-permute-done.1 = f32[2,8,128]{2,1,0:T(8,128)S(1)} collective-permute-done((f32[2,8,128]{2,1,0:T(8,128)S(1)}, f32[2,8,128]{2,1,0:T(8,128)S(1)}, u32[]{:S(2)}, u32[]{:S(2)}) %collective-permute-start.1) | collective-permute-done | bytes 8224 | tf_op jit(solution)/shard_map/ppermute | solution.py:444
  10.7 0.0 copy-done.3
  10.7 0.0 copy-done.1
  10.7 18.8 %all_to_all.15.own = f32[8,10,8,128]{3,2,1,0:T(8,128)S(1)} all-to-all(f32[8,10,8,128]{3,2,1,0:T(8,128)S(1)} %bitcast.18), channel_id=1, replica_groups=mesh['gx_0'=12,'gx_1'=2,'gy'=4,'gz'=8] {'gx_1','gy'}, dimensions={0} | all-to-all | bytes 655360 | tf_op jit(solution)/shard_map/all_to_all | solution.py:449
  29.7 1.3 %collective-permute-start.2 = (f32[68,8,128]{2,1,0:T(8,128)S(1)}, f32[68,8,128]{2,1,0:T(8,128)S(1)}, u32[]{:S(2)}, u32[]{:S(2)}) collective-permute-start(f32[68,8,128]{2,1,0:T(8,128)S(1)} %pad_maximum_fusion), channel_id=1, source_target_pairs={{0,64},{64,128},{128,192},{192,256},{256,320},{320,384},{384,448},... | collective-permute-start | bytes 835592 | tf_op jit(solution)/shard_map/ppermute | solution.py:451
  31.0 1.3 %collective-permute-start.3 = (f32[68,8,128]{2,1,0:T(8,128)S(1)}, f32[68,8,128]{2,1,0:T(8,128)S(1)}, u32[]{:S(2)}, u32[]{:S(2)}) collective-permute-start(f32[68,8,128]{2,1,0:T(8,128)S(1)} %pad_maximum_fusion.1), channel_id=1, source_target_pairs={{64,0},{128,64},{192,128},{256,192},{320,256},{384,320},{448,384},... | collective-permute-start | bytes 835592 | tf_op jit(solution)/shard_map/ppermute | solution.py:452
  32.4 0.1 stack.32.where_ref
  32.4 4.4 %collective-permute-done.2.low = f32[68,8,128]{2,1,0:T(8,128)S(1)} collective-permute-done((f32[68,8,128]{2,1,0:T(8,128)S(1)}, f32[68,8,128]{2,1,0:T(8,128)S(1)}, u32[]{:S(2)}, u32[]{:S(2)}) %collective-permute-start.2) | collective-permute-done | bytes 278560 | tf_op jit(solution)/shard_map/ppermute | solution.py:451
  36.8 3.9 %collective-permute-done.3.high = f32[68,8,128]{2,1,0:T(8,128)S(1)} collective-permute-done((f32[68,8,128]{2,1,0:T(8,128)S(1)}, f32[68,8,128]{2,1,0:T(8,128)S(1)}, u32[]{:S(2)}, u32[]{:S(2)}) %collective-permute-start.3) | collective-permute-done | bytes 278560 | tf_op jit(solution)/shard_map/ppermute | solution.py:452
  40.8 13.4 %powers.1 = (f32[4,8,8,128]{3,2,1,0:T(8,128)S(1)}, f32[9,8,8,128]{3,2,1,0:T(8,128)S(1)}, f32[5,8,8,128]{3,2,1,0:T(8,128)S(1)}, f32[16,128]{1,0:T(8,128)S(1)}) custom-call(s32[6]{0:T(128)S(1)} %stack.32.where_ref, f32[8,10,8,128]{3,2,1,0:T(8,128)S(1)} %all_to_all.15.own, f32[68,8,128]{2,1,0:T(8,128)S(1)} %collective-permute-done.2.low, ...), custom_call_target="tpu_custom_call" | custom-call | tf_op jit(solution)/shard_map/powers/pallas_call | solution.py:352
  54.2 3.2 %collective-permute-start.4 = (f32[9,8,8,128]{3,2,1,0:T(8,128)S(1)}, f32[9,8,8,128]{3,2,1,0:T(8,128)S(1)}, u32[]{:S(2)}, u32[]{:S(2)}) collective-permute-start(f32[9,8,8,128]{3,2,1,0:T(8,128)S(1)} %get-tuple-element.16), channel_id=1, source_target_pairs={{0,32},{32,0},{1,33},{33,1},{2,34},{34,2},{3,35},{35,3},{4,36},{36... | collective-permute-start | bytes 884744 | tf_op jit(solution)/shard_map/ppermute | solution.py:454
  57.3 1.2 %collective-permute-done.4.other = f32[9,8,8,128]{3,2,1,0:T(8,128)S(1)} collective-permute-done((f32[9,8,8,128]{3,2,1,0:T(8,128)S(1)}, f32[9,8,8,128]{3,2,1,0:T(8,128)S(1)}, u32[]{:S(2)}, u32[]{:S(2)}) %collective-permute-start.4) | collective-permute-done | bytes 294944 | tf_op jit(solution)/shard_map/ppermute | solution.py:454
  58.5 1.4 %products.1 = (f32[2,4,8,8,128]{4,3,2,1,0:T(8,128)}, f32[1,128]{1,0:T(1,128)S(1)}) custom-call(s32[6]{0:T(128)S(1)} %stack.32.where_ref, f32[4,8,8,128]{3,2,1,0:T(8,128)S(1)} %get-tuple-element.15.mine, f32[9,8,8,128]{3,2,1,0:T(8,128)S(1)} %collective-permute-done.4.other, f32[5,8,8,128]{3,2,1,0:T(8,128)S(1)} %get-tuple-element.17.images, ...), custom_call_target="tpu_custom_call" | custom-call | tf_op jit(solution)/shard_map/products/pallas_call | solution.py:374
  59.9 14.7 %all_to_all.16 = f32[32,1,128]{2,1,0:T(1,128)S(1)} all-to-all(f32[32,1,128]{2,1,0:T(1,128)S(1)} %broadcast_in_dim.10), channel_id=1, replica_groups=mesh['gx_0'=12,'gx_1'=2,'gy'=4,'gz'=8] {'gy','gz'}, dimensions={0} | all-to-all | bytes 32768 | tf_op jit(solution)/shard_map/all_to_all | solution.py:426
  74.7 25.9 %all_to_all.17.parts_ref = f32[24,1,128]{2,1,0:T(1,128)S(1)} all-to-all(f32[24,1,128]{2,1,0:T(1,128)S(1)} %broadcast_in_dim.11), channel_id=1, replica_groups=mesh['gx_0'=12,'gx_1'=2,'gy'=4,'gz'=8] {'gx_0','gx_1'}, dimensions={0} | all-to-all | bytes 24576 | tf_op jit(solution)/shard_map/all_to_all | solution.py:426
  100.6 0.7 totals.1
  (15 shorter events, 0.2 us)
Async XLA Ops:
  0.6 0.8 copy-start
  1.4 0.8 copy-start.2
  2.1 8.5 %copy-start.3 = (f32[8,8,128]{2,1,0:T(8,128)S(1)}, f32[8,8,128]{2,1,0:T(8,128)}, u32[]{:S(2)}) copy-start(f32[8,8,128]{2,1,0:T(8,128)} %residual.3) | copy-start | bytes 98308
  2.2 8.4 %copy-start.1 = (f32[8,8,128]{2,1,0:T(8,128)S(1)}, f32[8,8,128]{2,1,0:T(8,128)}, u32[]{:S(2)}) copy-start(f32[8,8,128]{2,1,0:T(8,128)} %direction.3) | copy-start | bytes 98308
  2.3 5.3 %collective-permute-start = (f32[2,8,128]{2,1,0:T(8,128)S(1)}, f32[2,8,128]{2,1,0:T(8,128)S(1)}, u32[]{:S(2)}, u32[]{:S(2)}) collective-permute-start(f32[2,8,128]{2,1,0:T(8,128)S(1)} %get-tuple-element.13), channel_id=1, source_target_pairs={{0,1},{1,2},{2,3},{3,4},{4,5},{5,6},{6,7},{8,9},{9,10},{10,11},{11... | collective-permute-start | bytes 24584 | tf_op jit(solution)/shard_map/ppermute | solution.py:443
  6.3 4.4 %collective-permute-start.1 = (f32[2,8,128]{2,1,0:T(8,128)S(1)}, f32[2,8,128]{2,1,0:T(8,128)S(1)}, u32[]{:S(2)}, u32[]{:S(2)}) collective-permute-start(f32[2,8,128]{2,1,0:T(8,128)S(1)} %get-tuple-element.14), channel_id=1, source_target_pairs={{1,0},{2,1},{3,2},{4,3},{5,4},{6,5},{7,6},{9,8},{10,9},{11,10},{12... | collective-permute-start | bytes 24584 | tf_op jit(solution)/shard_map/ppermute | solution.py:444
  29.7 7.2 %collective-permute-start.2 = (f32[68,8,128]{2,1,0:T(8,128)S(1)}, f32[68,8,128]{2,1,0:T(8,128)S(1)}, u32[]{:S(2)}, u32[]{:S(2)}) collective-permute-start(f32[68,8,128]{2,1,0:T(8,128)S(1)} %pad_maximum_fusion), channel_id=1, source_target_pairs={{0,64},{64,128},{128,192},{192,256},{256,320},{320,384},{384,448},... | collective-permute-start | bytes 835592 | tf_op jit(solution)/shard_map/ppermute | solution.py:451
  31.0 9.7 %collective-permute-start.3 = (f32[68,8,128]{2,1,0:T(8,128)S(1)}, f32[68,8,128]{2,1,0:T(8,128)S(1)}, u32[]{:S(2)}, u32[]{:S(2)}) collective-permute-start(f32[68,8,128]{2,1,0:T(8,128)S(1)} %pad_maximum_fusion.1), channel_id=1, source_target_pairs={{64,0},{128,64},{192,128},{256,192},{320,256},{384,320},{448,384},... | collective-permute-start | bytes 835592 | tf_op jit(solution)/shard_map/ppermute | solution.py:452
  54.2 4.4 %collective-permute-start.4 = (f32[9,8,8,128]{3,2,1,0:T(8,128)S(1)}, f32[9,8,8,128]{3,2,1,0:T(8,128)S(1)}, u32[]{:S(2)}, u32[]{:S(2)}) collective-permute-start(f32[9,8,8,128]{3,2,1,0:T(8,128)S(1)} %get-tuple-element.16), channel_id=1, source_target_pairs={{0,32},{32,0},{1,33},{33,1},{2,34},{34,2},{3,35},{35,3},{4,36},{36... | collective-permute-start | bytes 884744 | tf_op jit(solution)/shard_map/ppermute | solution.py:454

commit v3 on v2

--- a/solution.py
+++ b/solution.py
@@ -23,6 +23,7 @@
 LEAD = UNROLL + 6
 ORIGIN = LEAD + HALO
 C0, C1, CS = 117.0, 15.0, 1.0 / 729.0
+SUMS = (STEPS + 1) * (STEPS + 2) // 2 + STEPS + 1
 
 f32 = jnp.float32
 
@@ -31,21 +32,29 @@
     return lax.broadcasted_iota(jnp.int32, (8, 128), 1)
 
 
-def pack_kernel(direction, residual, up, down):
+def pack_kernel(direction, residual, up, down, buffer, semaphores):
+    copies = [
+        pltpu.make_async_copy(ref, buffer.at[k], semaphores.at[k])
+        for k, ref in enumerate((direction, residual))
+    ]
+    for copy in copies:
+        copy.start()
+    for copy in copies:
+        copy.wait()
     lane = lanes()
-    for k, ref in enumerate((direction, residual)):
+    for k in range(2):
         high = jnp.zeros((8, 128), f32)
         low = jnp.zeros((8, 128), f32)
         for p in range(BX):
             here = (lane >= STRIP * p) & (lane < STRIP * (p + 1))
-            v = ref[p]
+            v = buffer[k, p]
             high = jnp.where(here, pltpu.roll(v, (STRIP * p - (BZ - STRIP)) % 128, 1), high)
             low = jnp.where(here, pltpu.roll(v, STRIP * p, 1) if p else v, low)
         up[k] = high
         down[k] = low
 
 
-def powers_kernel(where_ref, own, low, high, mine, theirs, images, sums, *scratch):
+def powers_kernel(where_ref, own, low, high, residual, slab, theirs, sums, *scratch):
     fields = scratch[:5]
     flat, b_ref, g0_ref, g1_ref, g2_ref, x0_ref, x1_ref, x2_ref, zw, yw = scratch[5:]
     core, ix, iy, iz = where_ref[0], where_ref[1], where_ref[2], where_ref[3]
@@ -222,19 +231,27 @@
                     v = v * z_row(1, 6)
                 target[k, i, PAD : PAD + ROWS, :] = v
 
-        def turn(n, _, lo_b=lo_b):
-            i = lo_b + UNROLL * n
-            for u in range(UNROLL):
-                along_z(i + u - UNROLL)
-            for u in range(UNROLL):
-                along_y(i + u - UNROLL)
-            for u in range(UNROLL):
-                along_x(i + u - UNROLL - 2)
+        def ahead(i):
             for u in range(UNROLL):
                 image(i + u)
+
+        def behind(i):
+            for u in range(UNROLL):
+                along_z(i + u)
+            for u in range(UNROLL):
+                along_y(i + u)
+            for u in range(UNROLL):
+                along_x(i + u - 2)
+
+        def turn(n, _, lo_b=lo_b):
+            behind(lo_b + UNROLL * n)
+            ahead(lo_b + UNROLL * (n + 1))
             return 0
 
-        lax.fori_loop(0, -(-(hi_b - lo_b) // UNROLL) + 1, turn, 0)
+        turns = -(-(hi_b - lo_b) // UNROLL)
+        ahead(lo_b)
+        lax.fori_loop(0, turns - 1, turn, 0)
+        behind(lo_b + UNROLL * (turns - 1))
 
     def last_image(i):
         c, nc = around(fields[STEPS], i)[0]
@@ -248,38 +265,54 @@
     lax.fori_loop(0, 2, last_turn, 0)
 
     rows = pl.ds(pl.multiple_of(PAD + BY * iy, 8), BY)
-    flat_rows = pl.ds(pl.multiple_of(BY * iy, 8), BY)
-    for j in range(1, STEPS + 1):
-        mine[j - 1] = fields[j][0, pl.ds(ORIGIN + BX * core, BX), rows, :]
-        theirs[j - 1] = fields[j][0, pl.ds(ORIGIN + BX * (1 - core), BX), rows, :]
-    for j in range(STEPS + 1):
-        images[j] = flat[j, pl.ds(ORIGIN + BX * core, BX), flat_rows, :]
-        theirs[STEPS + j] = flat[j, pl.ds(ORIGIN + BX * (1 - core), BX), flat_rows, :]
+    for j in range(STEPS):
+        slab[j] = fields[j + 1][0, ORIGIN : ORIGIN + SLAB, PAD : PAD + ROWS, :]
+        theirs[BX * j : BX * (j + 1)] = fields[j + 1][0, pl.ds(ORIGIN + BX * (1 - core), BX), rows, :]
+    for x in range(SLAB):
+        for t in range(TILES):
+            theirs[BX * STEPS + TILES * x + t] = flat[STEPS, ORIGIN + x, BY * t : BY * (t + 1), :]
 
     pairs = [(a, b) for a in range(STEPS + 1) for b in range(a, STEPS + 1)]
-    totals = [jnp.zeros((8, 128), f32) for _ in pairs]
-    for x in range(SLAB):
-        fs = [fields[j][0, ORIGIN + x, rows, :] for j in range(STEPS + 1)]
-        im = [flat[j, ORIGIN + x, flat_rows, :] for j in range(STEPS + 1)]
-        totals = [total + fs[a] * im[b] for total, (a, b) in zip(totals, pairs)]
-    sums[...] = jnp.zeros((16, 128), f32)
+
+    def add_plane(x, carry):
+        i = ORIGIN + x
+        carry = list(carry)
+        for t in range(TILES):
+            fs = [fields[j][0, i, PAD + BY * t : PAD + BY * (t + 1), :] for j in range(STEPS + 1)]
+            im = [flat[j, i, BY * t : BY * (t + 1), :] for j in range(STEPS + 1)]
+            r = jnp.where(core == 0, residual[x, t], fs[0])
+            for n, (a, b) in enumerate(pairs):
+                carry[n] = carry[n] + fs[a] * im[b]
+            for a in range(STEPS + 1):
+                carry[len(pairs) + a] = carry[len(pairs) + a] + fs[a] * r
+        return tuple(carry)
+
+    totals = lax.fori_loop(0, SLAB, add_plane, tuple(jnp.zeros((8, 128), f32) for _ in range(SUMS)))
+    sums[...] = jnp.zeros((24, 128), f32)
     for n, total in enumerate(totals):
         sums[n : n + 1, :] = jnp.sum(total, axis=0, keepdims=True)
 
 
-def products_kernel(where_ref, mine, other, images, sums, direction, residual, powers, row, table):
+def products_kernel(where_ref, slab, other, sums, powers, row, table):
     north = where_ref[0] == 0
-    d, r = direction[...], residual[...]
-    own = [jnp.where(north, d, r)] + [mine[j] for j in range(STEPS)]
-    far = [jnp.where(north, r, d)] + [other[j] for j in range(STEPS)]
-    p = [d] + [jnp.where(north, own[j], far[j]) for j in range(1, STEPS + 1)]
-    z = [jnp.where(north, far[j], own[j]) for j in range(1, STEPS + 1)]
+    core, iy = where_ref[0], where_ref[2]
+    rows = pl.ds(pl.multiple_of(BY * iy, 8), BY)
     for j in range(STEPS):
-        powers[0, j] = p[j + 1]
-        powers[1, j] = z[j]
-
-    def fold(v):
-        return jnp.sum(jnp.sum(v, axis=0), axis=0, keepdims=True)
+        own = slab[j, pl.ds(BX * core, BX), rows, :]
+        far = other[BX * j : BX * (j + 1)]
+        powers[0, j] = jnp.where(north, own, far)
+        powers[1, j] = jnp.where(north, far, own)
+
+    def add_plane(x, carry):
+        carry = list(carry)
+        for t in range(TILES):
+            image = other[BX * STEPS + TILES * x + t]
+            for j in range(STEPS):
+                carry[j] = carry[j] + slab[j, x, BY * t : BY * (t + 1), :] * image
+        return tuple(carry)
+
+    cross = lax.fori_loop(0, SLAB, add_plane, tuple(jnp.zeros((8, 128), f32) for _ in range(STEPS)))
+    cross = [jnp.sum(v, axis=0, keepdims=True) for v in cross]
 
     zero = jnp.zeros((1, 128), f32)
     local = {}
@@ -288,22 +321,24 @@
         for b in range(a, STEPS + 1):
             local[a, b] = local[b, a] = sums[n : n + 1, :]
             n += 1
-    image = [jnp.where(north, images[a], other[STEPS + a]) for a in range(STEPS + 1)]
-    cross = [[fold(image[a] * z[b]) for b in range(STEPS)] for a in range(STEPS + 1)]
+    against = [sums[n + a : n + a + 1, :] for a in range(STEPS + 1)]
+    hankel = against[1:] + cross
     table[...] = jnp.zeros((128, 128), f32)
     size = 2 * STEPS + 1
     for a in range(size):
         for b in range(size):
-            if a <= STEPS and b <= STEPS:
+            if a > STEPS and b > STEPS:
+                v = jnp.where(north, zero, local[a - STEPS, b - STEPS])
+            elif a <= STEPS and b <= STEPS:
                 v = jnp.where(north, local[a, b], zero)
-            elif a > STEPS and b > STEPS:
-                v = jnp.where(north, zero, local[a - STEPS, b - STEPS])
             else:
-                v = cross[min(a, b)][max(a, b) - STEPS - 1]
+                v = jnp.where(north, hankel[a + b - STEPS - 1], zero)
             table[size * a + b : size * a + b + 1, :] = v
-    for a, v in enumerate(p + z):
-        at = size * size + a
-        table[at : at + 1, :] = fold(v * r)
+    for a in range(STEPS + 1):
+        table[size * size + a : size * size + a + 1, :] = jnp.where(north, against[a], zero)
+        if a:
+            at = size * size + STEPS + a
+            table[at : at + 1, :] = jnp.where(north, zero, against[a])
     row[...] = lax.dot_general(
         jnp.ones((8, 128), f32),
         table[...],
@@ -338,26 +373,26 @@
 def pack(direction, residual):
     return pl.pallas_call(
         pack_kernel,
-        in_specs=[VMEM, VMEM],
+        in_specs=[pl.BlockSpec(memory_space=pltpu.HBM)] * 2,
         out_specs=[VMEM, VMEM],
         out_shape=[shaped(2, 8, 128), shaped(2, 8, 128)],
+        scratch_shapes=[pltpu.VMEM((2, BX, 8, 128), f32), pltpu.SemaphoreType.DMA((2,))],
         compiler_params=pltpu.CompilerParams(vmem_limit_bytes=2 * 1024 * 1024),
         name="pack",
     )(direction, residual)
 
 
-def powers_of(where, own, low, high, interpret=False):
+def powers_of(where, own, low, high, residual, interpret=False):
     padded = (2, PLANES + 2 * LEAD, ROWS + 2 * PAD, 128)
     plain = (2, PLANES + 2 * LEAD, ROWS, 128)
     return pl.pallas_call(
         powers_kernel,
-        in_specs=[SMEM, VMEM, VMEM, VMEM],
-        out_specs=[VMEM] * 4,
+        in_specs=[SMEM, VMEM, VMEM, VMEM, VMEM],
+        out_specs=[VMEM] * 3,
         out_shape=[
-            shaped(STEPS, 8, 8, 128),
-            shaped(2 * STEPS + 1, 8, 8, 128),
-            shaped(STEPS + 1, 8, 8, 128),
-            shaped(16, 128),
+            shaped(STEPS, SLAB, ROWS, 128),
+            shaped(BX * STEPS + TILES * SLAB, 8, 128),
+            shaped(24, 128),
         ],
         scratch_shapes=[pltpu.VMEM(padded, f32)] * 5
         + [pltpu.VMEM((STEPS + 1, PLANES + 2 * LEAD, ROWS, 128), f32)]
@@ -367,20 +402,20 @@
         compiler_params=pltpu.CompilerParams(vmem_limit_bytes=44 * 1024 * 1024),
         interpret=interpret,
         name="powers",
-    )(where, own, low, high)
-
-
-def products(where, mine, other, images, sums, direction, residual, interpret=False):
+    )(where, own, low, high, residual)
+
+
+def products(where, slab, other, sums, interpret=False):
     return pl.pallas_call(
         products_kernel,
-        in_specs=[SMEM] + [VMEM] * 6,
+        in_specs=[SMEM] + [VMEM] * 3,
         out_specs=[VMEM, VMEM],
         out_shape=[shaped(2, STEPS, 8, 8, 128), shaped(1, 128)],
         scratch_shapes=[pltpu.VMEM((128, 128), f32)],
         interpret=interpret,
-        compiler_params=pltpu.CompilerParams(vmem_limit_bytes=2 * 1024 * 1024),
+        compiler_params=pltpu.CompilerParams(vmem_limit_bytes=4 * 1024 * 1024),
         name="products",
-    )(where, mine, other, images, sums, direction, residual)
+    )(where, slab, other, sums)
 
 
 def totals(parts, scale, interpret=False):
@@ -450,11 +485,13 @@
     send_up, send_down = x_messages(own)
     low = lax.ppermute(send_up, "gx_0", forward(nx))
     high = lax.ppermute(send_down, "gx_0", backward(nx))
-    mine, theirs, images, sums = powers_of(where, own, low, high)
+    blocks = own[:, :BX].reshape(2, TILES, BX, 8, 128).swapaxes(1, 2).reshape(SLAB, TILES, 8, 128)
+    across = lax.ppermute(blocks, "gx_1", [(1, 0)])
+    slab, theirs, sums = powers_of(where, own, low, high, across)
     other = lax.ppermute(theirs, "gx_1", [(0, 1), (1, 0)])
-    powers, row = products(where, mine, other, images, sums, direction, residual)
-    row = jnp.sum(everyone(row, ("gy", "gz"), ny * nz), axis=0)
-    parts = everyone(row, GX, 2 * nx)
+    powers, row = products(where, slab, other, sums)
+    row = jnp.sum(everyone(row, ("gx_1", "gz"), 2 * nz), axis=0)
+    parts = everyone(row, "gx_0", nx)
     cells = float(2 * nx * BX * ny * BY * nz * BZ)
     gram, projections = totals(parts, 1.0 / cells)
     return powers, gram, projections.reshape(-1)

time: 102 us -> 96.7 us (0.948)
  blocking collectives: 59.5 us -> 54.9 us
  starting transfers between devices: 11.1 us -> 13.4 us
  waiting for transfers between devices: 12.6 us -> 10.3 us
    all_to_all x2, blocking collectives: 40.6 us -> 36 us  [everyone(): lax.all_to_all(jnp.broadcast_to(x[None], (count,) + x.shape), axes, 0, 0)]
    ppermute x1, waiting for transfers between devices: 4.39 us -> 0.99 us  [local(): low = lax.ppermute(send_up, 'gx_0', forward(nx))]
    ppermute x0 -> x1, starting transfers between devices: none -> 2.31 us  [local(): across = lax.ppermute(blocks, 'gx_1', [(1, 0)])]
    ppermute x0 -> x1, waiting for transfers between devices: none -> 1.03 us  [local(): across = lax.ppermute(blocks, 'gx_1', [(1, 0)])]
  transfers between devices with their start and end apart: 5 -> 6, of which waited for: 4 -> 5; matrix products, arithmetic and copies ran while one was open for 0% -> 0% of each run, Pallas kernels for 0% -> 0%
where the time goes in v3:
time: 96.7 us; the launch traced here: 96.2 us
  blocking collectives  54.9 us (57%)
  Pallas kernels  15 us (16%)
  starting transfers between devices  13.4 us (14%)
  waiting for transfers between devices  10.3 us (11%)
  local copies, waits for them, and re-layouts  1.73 us (2%)
    all_to_all x2, blocking collectives, everyone(): lax.all_to_all(jnp.broadcast_to(x[None], (count,) + x.shape), axes, 0, 0)  36 us
    all_to_all x1, blocking collectives, local(): lax.all_to_all(message.reshape((2 * TILES,) + message.shape[2:]), ('gx_1'...  18.8 us
    pallas_call x1, Pallas kernels, powers_of(): pl.pallas_call(powers_kernel, in_specs=[SMEM, VMEM, VMEM, VMEM, VMEM], ou...  12.7 us
    ppermute x1, starting transfers between devices, local(): left = lax.ppermute(up, 'gz', forward(nz))  4.02 us
    ppermute x1, waiting for transfers between devices, local(): high = lax.ppermute(send_down, 'gx_0', backward(nx))  3.92 us
    ppermute x1, starting transfers between devices, local(): other = lax.ppermute(theirs, 'gx_1', [(0, 1), (1, 0)])  3.16 us
    ppermute x1, waiting for transfers between devices, local(): right = lax.ppermute(down, 'gz', backward(nz))  3.07 us
    ppermute x1, starting transfers between devices, local(): across = lax.ppermute(blocks, 'gx_1', [(1, 0)])  2.31 us
  transfers between devices with their start and end apart: 6, of which 5 were waited for; matrix products, arithmetic and copies ran while one was open for 0% of the time, Pallas kernels for 0%

profile of v3, /device:TPU:1, one launch (start us, length us, event | category | flops | bytes accessed | tf_op | source)
XLA Modules:
  0.0 96.2 jit_solution(10918677404774958679)
XLA Ops:
  0.6 0.0 copy-start
  0.6 0.7 copy-done
  1.4 0.0 copy-start.2
  1.4 0.8 copy-done.2
  2.1 0.0 copy-start.3
  2.2 0.2 pack.1
  2.3 0.0 copy-start.1
  2.3 4.0 %collective-permute-start = (f32[2,8,128]{2,1,0:T(8,128)S(1)}, f32[2,8,128]{2,1,0:T(8,128)S(1)}, u32[]{:S(2)}, u32[]{:S(2)}) collective-permute-start(f32[2,8,128]{2,1,0:T(8,128)S(1)} %get-tuple-element.12), channel_id=1, source_target_pairs={{0,1},{1,2},{2,3},{3,4},{4,5},{5,6},{6,7},{8,9},{9,10},{10,11},{11... | collective-permute-start | bytes 24584 | tf_op jit(solution)/shard_map/ppermute | solution.py:478
  6.4 1.3 %collective-permute-start.1 = (f32[2,8,128]{2,1,0:T(8,128)S(1)}, f32[2,8,128]{2,1,0:T(8,128)S(1)}, u32[]{:S(2)}, u32[]{:S(2)}) collective-permute-start(f32[2,8,128]{2,1,0:T(8,128)S(1)} %get-tuple-element.13), channel_id=1, source_target_pairs={{1,0},{2,1},{3,2},{4,3},{5,4},{6,5},{7,6},{9,8},{10,9},{11,10},{12... | collective-permute-start | bytes 24584 | tf_op jit(solution)/shard_map/ppermute | solution.py:479
  7.7 0.0 collective-permute-done
  7.7 3.1 %collective-permute-done.1 = f32[2,8,128]{2,1,0:T(8,128)S(1)} collective-permute-done((f32[2,8,128]{2,1,0:T(8,128)S(1)}, f32[2,8,128]{2,1,0:T(8,128)S(1)}, u32[]{:S(2)}, u32[]{:S(2)}) %collective-permute-start.1) | collective-permute-done | bytes 8224 | tf_op jit(solution)/shard_map/ppermute | solution.py:479
  10.8 0.0 copy-done.3
  10.8 0.0 copy-done.1
  10.8 18.8 %all_to_all.15.own = f32[8,10,8,128]{3,2,1,0:T(8,128)S(1)} all-to-all(f32[8,10,8,128]{3,2,1,0:T(8,128)S(1)} %bitcast.22), channel_id=1, replica_groups=mesh['gx_0'=12,'gx_1'=2,'gy'=4,'gz'=8] {'gx_1','gy'}, dimensions={0} | all-to-all | bytes 655360 | tf_op jit(solution)/shard_map/all_to_all | solution.py:484
  29.7 1.3 %collective-permute-start.2 = (f32[68,8,128]{2,1,0:T(8,128)S(1)}, f32[68,8,128]{2,1,0:T(8,128)S(1)}, u32[]{:S(2)}, u32[]{:S(2)}) collective-permute-start(f32[68,8,128]{2,1,0:T(8,128)S(1)} %pad_maximum_fusion), channel_id=1, source_target_pairs={{0,64},{64,128},{128,192},{192,256},{256,320},{320,384},{384,448},... | collective-permute-start | bytes 835592 | tf_op jit(solution)/shard_map/ppermute | solution.py:486
  31.1 1.3 %collective-permute-start.3 = (f32[68,8,128]{2,1,0:T(8,128)S(1)}, f32[68,8,128]{2,1,0:T(8,128)S(1)}, u32[]{:S(2)}, u32[]{:S(2)}) collective-permute-start(f32[68,8,128]{2,1,0:T(8,128)S(1)} %pad_maximum_fusion.1), channel_id=1, source_target_pairs={{64,0},{128,64},{192,128},{256,192},{320,256},{384,320},{448,384},... | collective-permute-start | bytes 835592 | tf_op jit(solution)/shard_map/ppermute | solution.py:487
  32.5 2.3 %collective-permute-start.4 = (f32[16,4,8,128]{3,2,1,0:T(8,128)S(1)}, f32[16,4,8,128]{3,2,1,0:T(8,128)S(1)}, u32[]{:S(2)}, u32[]{:S(2)}) collective-permute-start(f32[16,4,8,128]{3,2,1,0:T(8,128)S(1)} %bitcast.28), channel_id=1, source_target_pairs={{32,0},{33,1},{34,2},{35,3},{36,4},{37,5},{38,6},{39,7},{40,8},{41... | collective-permute-start | bytes 786440 | tf_op jit(solution)/shard_map/ppermute | solution.py:489
  34.8 0.1 stack.32.where_ref
  34.9 1.0 %collective-permute-done.4.residual = f32[16,4,8,128]{3,2,1,0:T(8,128)S(1)} collective-permute-done((f32[16,4,8,128]{3,2,1,0:T(8,128)S(1)}, f32[16,4,8,128]{3,2,1,0:T(8,128)S(1)}, u32[]{:S(2)}, u32[]{:S(2)}) %collective-permute-start.4) | collective-permute-done | bytes 262176 | tf_op jit(solution)/shard_map/ppermute | solution.py:489
  35.9 1.0 %collective-permute-done.2.low = f32[68,8,128]{2,1,0:T(8,128)S(1)} collective-permute-done((f32[68,8,128]{2,1,0:T(8,128)S(1)}, f32[68,8,128]{2,1,0:T(8,128)S(1)}, u32[]{:S(2)}, u32[]{:S(2)}) %collective-permute-start.2) | collective-permute-done | bytes 278560 | tf_op jit(solution)/shard_map/ppermute | solution.py:486
  36.9 3.9 %collective-permute-done.3.high = f32[68,8,128]{2,1,0:T(8,128)S(1)} collective-permute-done((f32[68,8,128]{2,1,0:T(8,128)S(1)}, f32[68,8,128]{2,1,0:T(8,128)S(1)}, u32[]{:S(2)}, u32[]{:S(2)}) %collective-permute-start.3) | collective-permute-done | bytes 278560 | tf_op jit(solution)/shard_map/ppermute | solution.py:487
  40.8 12.7 %powers.1 = (f32[4,16,32,128]{3,2,1,0:T(8,128)S(1)}, f32[96,8,128]{2,1,0:T(8,128)S(1)}, f32[24,128]{1,0:T(8,128)S(1)}) custom-call(s32[6]{0:T(128)S(1)} %stack.32.where_ref, f32[8,10,8,128]{3,2,1,0:T(8,128)S(1)} %all_to_all.15.own, f32[68,8,128]{2,1,0:T(8,128)S(1)} %collective-permute-done.2.low, f32[68,8,128]{2,1,0:T(8,128)S(1)} %collective-permute-done.3.high, ...), custom_call_target="tpu_custom_call" | custom-call | tf_op jit(solution)/shard_map/powers/pallas_call | solution.py:388
  53.5 3.2 %collective-permute-start.5 = (f32[96,8,128]{2,1,0:T(8,128)S(1)}, f32[96,8,128]{2,1,0:T(8,128)S(1)}, u32[]{:S(2)}, u32[]{:S(2)}) collective-permute-start(f32[96,8,128]{2,1,0:T(8,128)S(1)} %get-tuple-element.15), channel_id=1, source_target_pairs={{0,32},{32,0},{1,33},{33,1},{2,34},{34,2},{3,35},{35,3},{4,36},{36... | collective-permute-start | bytes 1179656 | tf_op jit(solution)/shard_map/ppermute | solution.py:491
  56.7 1.3 %collective-permute-done.5.other = f32[96,8,128]{2,1,0:T(8,128)S(1)} collective-permute-done((f32[96,8,128]{2,1,0:T(8,128)S(1)}, f32[96,8,128]{2,1,0:T(8,128)S(1)}, u32[]{:S(2)}, u32[]{:S(2)}) %collective-permute-start.5) | collective-permute-done | bytes 393248 | tf_op jit(solution)/shard_map/ppermute | solution.py:491
  58.0 1.4 %products.1 = (f32[2,4,8,8,128]{4,3,2,1,0:T(8,128)}, f32[1,128]{1,0:T(1,128)S(1)}) custom-call(s32[6]{0:T(128)S(1)} %stack.32.where_ref, f32[4,16,32,128]{3,2,1,0:T(8,128)S(1)} %get-tuple-element.14.slab, f32[96,8,128]{2,1,0:T(8,128)S(1)} %collective-permute-done.5.other, f32[24,128]{1,0:T(8,128)S(1)} %get-tuple-element.16.sums), custom_call_target="tpu_custom_call" | custom-call | tf_op jit(solution)/shard_map/products/pallas_call | solution.py:409
  59.5 12.7 %all_to_all.16 = f32[16,1,128]{2,1,0:T(1,128)S(1)} all-to-all(f32[16,1,128]{2,1,0:T(1,128)S(1)} %broadcast_in_dim.10), channel_id=1, replica_groups=mesh['gx_0'=12,'gx_1'=2,'gy'=4,'gz'=8] {'gx_1','gz'}, dimensions={0} | all-to-all | bytes 16384 | tf_op jit(solution)/shard_map/all_to_all | solution.py:461
  72.2 23.3 %all_to_all.17.parts_ref = f32[12,1,128]{2,1,0:T(1,128)S(1)} all-to-all(f32[12,1,128]{2,1,0:T(1,128)S(1)} %broadcast_in_dim.11), channel_id=1, replica_groups=mesh['gx_0'=12,'gx_1'=2,'gy'=4,'gz'=8] {'gx_0'}, dimensions={0} | all-to-all | bytes 12288 | tf_op jit(solution)/shard_map/all_to_all | solution.py:461
  95.5 0.7 totals.1
  (17 shorter events, 0.2 us)
Async XLA Ops:
  0.6 0.8 copy-start
  1.4 0.8 copy-start.2
  2.1 8.6 %copy-start.3 = (f32[8,8,128]{2,1,0:T(8,128)S(1)}, f32[8,8,128]{2,1,0:T(8,128)}, u32[]{:S(2)}) copy-start(f32[8,8,128]{2,1,0:T(8,128)} %residual.1) | copy-start | bytes 98308
  2.3 8.4 %copy-start.1 = (f32[8,8,128]{2,1,0:T(8,128)S(1)}, f32[8,8,128]{2,1,0:T(8,128)}, u32[]{:S(2)}) copy-start(f32[8,8,128]{2,1,0:T(8,128)} %direction.1) | copy-start | bytes 98308
  2.3 5.3 %collective-permute-start = (f32[2,8,128]{2,1,0:T(8,128)S(1)}, f32[2,8,128]{2,1,0:T(8,128)S(1)}, u32[]{:S(2)}, u32[]{:S(2)}) collective-permute-start(f32[2,8,128]{2,1,0:T(8,128)S(1)} %get-tuple-element.12), channel_id=1, source_target_pairs={{0,1},{1,2},{2,3},{3,4},{4,5},{5,6},{6,7},{8,9},{9,10},{10,11},{11... | collective-permute-start | bytes 24584 | tf_op jit(solution)/shard_map/ppermute | solution.py:478
  6.4 4.4 %collective-permute-start.1 = (f32[2,8,128]{2,1,0:T(8,128)S(1)}, f32[2,8,128]{2,1,0:T(8,128)S(1)}, u32[]{:S(2)}, u32[]{:S(2)}) collective-permute-start(f32[2,8,128]{2,1,0:T(8,128)S(1)} %get-tuple-element.13), channel_id=1, source_target_pairs={{1,0},{2,1},{3,2},{4,3},{5,4},{6,5},{7,6},{9,8},{10,9},{11,10},{12... | collective-permute-start | bytes 24584 | tf_op jit(solution)/shard_map/ppermute | solution.py:479
  29.7 7.2 %collective-permute-start.2 = (f32[68,8,128]{2,1,0:T(8,128)S(1)}, f32[68,8,128]{2,1,0:T(8,128)S(1)}, u32[]{:S(2)}, u32[]{:S(2)}) collective-permute-start(f32[68,8,128]{2,1,0:T(8,128)S(1)} %pad_maximum_fusion), channel_id=1, source_target_pairs={{0,64},{64,128},{128,192},{192,256},{256,320},{320,384},{384,448},... | collective-permute-start | bytes 835592 | tf_op jit(solution)/shard_map/ppermute | solution.py:486
  31.1 9.7 %collective-permute-start.3 = (f32[68,8,128]{2,1,0:T(8,128)S(1)}, f32[68,8,128]{2,1,0:T(8,128)S(1)}, u32[]{:S(2)}, u32[]{:S(2)}) collective-permute-start(f32[68,8,128]{2,1,0:T(8,128)S(1)} %pad_maximum_fusion.1), channel_id=1, source_target_pairs={{64,0},{128,64},{192,128},{256,192},{320,256},{384,320},{448,384},... | collective-permute-start | bytes 835592 | tf_op jit(solution)/shard_map/ppermute | solution.py:487
  32.5 3.5 %collective-permute-start.4 = (f32[16,4,8,128]{3,2,1,0:T(8,128)S(1)}, f32[16,4,8,128]{3,2,1,0:T(8,128)S(1)}, u32[]{:S(2)}, u32[]{:S(2)}) collective-permute-start(f32[16,4,8,128]{3,2,1,0:T(8,128)S(1)} %bitcast.28), channel_id=1, source_target_pairs={{32,0},{33,1},{34,2},{35,3},{36,4},{37,5},{38,6},{39,7},{40,8},{41... | collective-permute-start | bytes 786440 | tf_op jit(solution)/shard_map/ppermute | solution.py:489
  53.5 4.5 %collective-permute-start.5 = (f32[96,8,128]{2,1,0:T(8,128)S(1)}, f32[96,8,128]{2,1,0:T(8,128)S(1)}, u32[]{:S(2)}, u32[]{:S(2)}) collective-permute-start(f32[96,8,128]{2,1,0:T(8,128)S(1)} %get-tuple-element.15), channel_id=1, source_target_pairs={{0,32},{32,0},{1,33},{33,1},{2,34},{34,2},{3,35},{35,3},{4,36},{36... | collective-permute-start | bytes 1179656 | tf_op jit(solution)/shard_map/ppermute | solution.py:491

commit v4 on v3

--- a/solution.py
+++ b/solution.py
@@ -17,10 +17,10 @@
 PAD = 8
 PLANES = SLAB + 2 * HALO
 NB = 10
-SHORT = HALO - BX + 2
+SHORT = HALO - BX + 1
 MSG = TILES * (NB + SHORT)
-UNROLL = 4
-LEAD = UNROLL + 6
+TURN = (10, 12, 14, 11)
+LEAD = 6
 ORIGIN = LEAD + HALO
 C0, C1, CS = 117.0, 15.0, 1.0 / 729.0
 SUMS = (STEPS + 1) * (STEPS + 2) // 2 + STEPS + 1
@@ -121,10 +121,10 @@
             left, right = own[TILES * c + t, BX], own[TILES * c + t, BX + 1]
             for p in range(BX):
                 place(BX * c + p, t, own[TILES * c + t, p], left, right)
-        n = SHORT - 2
+        n = SHORT - 1
         base = SHORT * t
         for p in range(n):
-            place(p - HALO, t, low[base + p], low[base + n], low[base + n + 1])
+            place(p - HALO, t, low[base + p], low[base + n], low[base + n])
         base = SHORT * TILES + NB * t
         for p in range(BX):
             place(p - BX, t, low[base + p], low[base + BX], low[base + BX + 1])
@@ -133,7 +133,7 @@
             place(SLAB + p, t, high[base + p], high[base + BX], high[base + BX + 1])
         base = NB * TILES + SHORT * t
         for p in range(n):
-            place(SLAB + BX + p, t, high[base + p], high[base + n], high[base + n + 1])
+            place(SLAB + BX + p, t, high[base + p], high[base + n], high[base + n])
 
     lane_row = lax.broadcasted_iota(jnp.int32, (ROWS, 128), 1)
 
@@ -231,27 +231,21 @@
                     v = v * z_row(1, 6)
                 target[k, i, PAD : PAD + ROWS, :] = v
 
-        def ahead(i):
-            for u in range(UNROLL):
+        count = TURN[step]
+
+        def turn(n, _, lo_b=lo_b, count=count):
+            i = lo_b + count * n
+            for u in range(count):
                 image(i + u)
-
-        def behind(i):
-            for u in range(UNROLL):
+            for u in range(count):
                 along_z(i + u)
-            for u in range(UNROLL):
+            for u in range(count):
                 along_y(i + u)
-            for u in range(UNROLL):
+            for u in range(count):
                 along_x(i + u - 2)
-
-        def turn(n, _, lo_b=lo_b):
-            behind(lo_b + UNROLL * n)
-            ahead(lo_b + UNROLL * (n + 1))
             return 0
 
-        turns = -(-(hi_b - lo_b) // UNROLL)
-        ahead(lo_b)
-        lax.fori_loop(0, turns - 1, turn, 0)
-        behind(lo_b + UNROLL * (turns - 1))
+        lax.fori_loop(0, -(-(hi_b - lo_b) // count), turn, 0)
 
     def last_image(i):
         c, nc = around(fields[STEPS], i)[0]
@@ -293,15 +287,19 @@
         sums[n : n + 1, :] = jnp.sum(total, axis=0, keepdims=True)
 
 
-def products_kernel(where_ref, slab, other, sums, powers, row, table):
+def products_kernel(where_ref, slab, other, sums, powers, row, table, semaphores):
     north = where_ref[0] == 0
     core, iy = where_ref[0], where_ref[2]
     rows = pl.ds(pl.multiple_of(BY * iy, 8), BY)
+    copies = [
+        pltpu.make_async_copy(slab.at[:, pl.ds(BX * core, BX), rows, :], powers.at[core], semaphores.at[STEPS])
+    ]
     for j in range(STEPS):
-        own = slab[j, pl.ds(BX * core, BX), rows, :]
-        far = other[BX * j : BX * (j + 1)]
-        powers[0, j] = jnp.where(north, own, far)
-        powers[1, j] = jnp.where(north, far, own)
+        copies.append(
+            pltpu.make_async_copy(other.at[BX * j : BX * (j + 1)], powers.at[1 - core, j], semaphores.at[j])
+        )
+    for copy in copies:
+        copy.start()
 
     def add_plane(x, carry):
         carry = list(carry)
@@ -346,6 +344,8 @@
         precision=lax.Precision.HIGHEST,
         preferred_element_type=f32,
     )[0:1, :]
+    for copy in copies:
+        copy.wait()
 
 
 def total_kernel(parts, gram, projections, *, scale):
@@ -409,9 +409,9 @@
     return pl.pallas_call(
         products_kernel,
         in_specs=[SMEM] + [VMEM] * 3,
-        out_specs=[VMEM, VMEM],
-        out_shape=[shaped(2, STEPS, 8, 8, 128), shaped(1, 128)],
-        scratch_shapes=[pltpu.VMEM((128, 128), f32)],
+        out_specs=[pl.BlockSpec(memory_space=pltpu.HBM), VMEM],
+        out_shape=[shaped(2, STEPS, BX, 8, 128), shaped(1, 128)],
+        scratch_shapes=[pltpu.VMEM((128, 128), f32), pltpu.SemaphoreType.DMA((STEPS + 1,))],
         interpret=interpret,
         compiler_params=pltpu.CompilerParams(vmem_limit_bytes=4 * 1024 * 1024),
         name="products",
@@ -439,14 +439,36 @@
     return jnp.concatenate([cells, left[None], right[None]], axis=0)
 
 
-def x_messages(own):
-    n = SHORT - 2
-    first, second = own[:TILES], own[TILES:]
-    flat = lambda v: v.reshape(-1, 8, 128)
-    up = jnp.concatenate([flat(first[:, BX - n :]), flat(second)], axis=0)
-    short = jnp.concatenate([second[:, :n], second[:, BX:]], axis=1)
-    down = jnp.concatenate([flat(first), flat(short)], axis=0)
-    return up, down
+def messages_kernel(own, up, down, blocks):
+    n = SHORT - 1
+    low_half = lanes() % STRIP < STRIP // 2
+    for t in range(TILES):
+        first, second = own.at[t], own.at[TILES + t]
+        far = SHORT * t
+        up[far : far + n] = first[BX - n : BX]
+        up[far + n] = jnp.where(low_half, first[BX + 1], first[BX])
+        near = TILES * SHORT + NB * t
+        up[near : near + NB] = second[...]
+        near = NB * t
+        down[near : near + NB] = first[...]
+        far = TILES * NB + SHORT * t
+        down[far : far + n] = second[0:n]
+        down[far + n] = jnp.where(low_half, second[BX + 1], second[BX])
+        for p in range(BX):
+            blocks[p, t] = first[p]
+            blocks[BX + p, t] = second[p]
+
+
+def x_messages(own, interpret=False):
+    return pl.pallas_call(
+        messages_kernel,
+        in_specs=[VMEM],
+        out_specs=[VMEM] * 3,
+        out_shape=[shaped(MSG, 8, 128), shaped(MSG, 8, 128), shaped(SLAB, TILES, 8, 128)],
+        compiler_params=pltpu.CompilerParams(vmem_limit_bytes=2 * 1024 * 1024),
+        interpret=interpret,
+        name="messages",
+    )(own)
 
 
 def forward(n):
@@ -474,7 +496,10 @@
             jnp.where(iz < nz - 1, 1, 0),
         ]
     ).astype(jnp.int32)
-    up, down = pack(direction, residual)
+    up, down = pack(
+        pltpu.with_memory_space_constraint(direction, pltpu.HBM),
+        pltpu.with_memory_space_constraint(residual, pltpu.HBM),
+    )
     left = lax.ppermute(up, "gz", forward(nz))
     right = lax.ppermute(down, "gz", backward(nz))
     message = jnp.stack(
@@ -482,10 +507,9 @@
     )
     message = jnp.broadcast_to(message[:, None], (2, TILES) + message.shape[1:])
     own = lax.all_to_all(message.reshape((2 * TILES,) + message.shape[2:]), ("gx_1", "gy"), 0, 0)
-    send_up, send_down = x_messages(own)
+    send_up, send_down, blocks = x_messages(own)
     low = lax.ppermute(send_up, "gx_0", forward(nx))
     high = lax.ppermute(send_down, "gx_0", backward(nx))
-    blocks = own[:, :BX].reshape(2, TILES, BX, 8, 128).swapaxes(1, 2).reshape(SLAB, TILES, 8, 128)
     across = lax.ppermute(blocks, "gx_1", [(1, 0)])
     slab, theirs, sums = powers_of(where, own, low, high, across)
     other = lax.ppermute(theirs, "gx_1", [(0, 1), (1, 0)])

time: 96.7 us -> 95.1 us (0.983)
  local copies, waits for them, and re-layouts: 1.73 us -> 0.14 us
    unnamed x8 -> x4, local copies, waits for them, and re-layouts: 1.52 us -> 0.01 us
    ppermute x1, waiting for transfers between devices: 1.03 us -> 0.01 us  [local(): across = lax.ppermute(blocks, 'gx_1', [(1, 0)])]
  transfers between devices with their start and end apart: 6 -> 6, of which waited for: 5 -> 4; matrix products, arithmetic and copies ran while one was open for 0% -> 0% of each run, Pallas kernels for 0% -> 0%
where the time goes in v4:
time: 95.1 us; the launch traced here: 94.6 us
  blocking collectives  54.9 us (58%)
  Pallas kernels  15.4 us (16%)
  starting transfers between devices  13.4 us (14%)
  waiting for transfers between devices  10 us (11%)
    all_to_all x2, blocking collectives, everyone(): lax.all_to_all(jnp.broadcast_to(x[None], (count,) + x.shape), axes, 0, 0)  36 us
    all_to_all x1, blocking collectives, local(): lax.all_to_all(message.reshape((2 * TILES,) + message.shape[2:]), ('gx_1'...  18.8 us
    pallas_call x1, Pallas kernels, powers_of(): pl.pallas_call(powers_kernel, in_specs=[SMEM, VMEM, VMEM, VMEM, VMEM], ou...  12.4 us
    ppermute x1, starting transfers between devices, local(): left = lax.ppermute(up, 'gz', forward(nz))  4.02 us
    ppermute x1, waiting for transfers between devices, local(): high = lax.ppermute(send_down, 'gx_0', backward(nx))  3.85 us
    ppermute x1, starting transfers between devices, local(): other = lax.ppermute(theirs, 'gx_1', [(0, 1), (1, 0)])  3.16 us
    ppermute x1, waiting for transfers between devices, local(): right = lax.ppermute(down, 'gz', backward(nz))  3.07 us
    ppermute x1, starting transfers between devices, local(): across = lax.ppermute(blocks, 'gx_1', [(1, 0)])  2.31 us
  transfers between devices with their start and end apart: 6, of which 4 were waited for; matrix products, arithmetic and copies ran while one was open for 0% of the time, Pallas kernels for 0%

profile of v4, /device:TPU:1, one launch (start us, length us, event | category | flops | bytes accessed | tf_op | source)
XLA Modules:
  0.0 94.6 jit_solution(14725140624587673930)
XLA Ops:
  0.6 0.0 copy-start.1
  0.6 0.9 pack.1
  1.6 0.0 copy-start
  1.6 4.0 %collective-permute-start = (f32[2,8,128]{2,1,0:T(8,128)S(1)}, f32[2,8,128]{2,1,0:T(8,128)S(1)}, u32[]{:S(2)}, u32[]{:S(2)}) collective-permute-start(f32[2,8,128]{2,1,0:T(8,128)S(1)} %get-tuple-element.15), channel_id=1, source_target_pairs={{0,1},{1,2},{2,3},{3,4},{4,5},{5,6},{6,7},{8,9},{9,10},{10,11},{11... | collective-permute-start | bytes 24584 | tf_op jit(solution)/shard_map/ppermute | solution.py:503
  5.6 1.3 %collective-permute-start.1 = (f32[2,8,128]{2,1,0:T(8,128)S(1)}, f32[2,8,128]{2,1,0:T(8,128)S(1)}, u32[]{:S(2)}, u32[]{:S(2)}) collective-permute-start(f32[2,8,128]{2,1,0:T(8,128)S(1)} %get-tuple-element.16), channel_id=1, source_target_pairs={{1,0},{2,1},{3,2},{4,3},{5,4},{6,5},{7,6},{9,8},{10,9},{11,10},{12... | collective-permute-start | bytes 24584 | tf_op jit(solution)/shard_map/ppermute | solution.py:504
  6.9 0.0 collective-permute-done
  6.9 3.1 %collective-permute-done.1 = f32[2,8,128]{2,1,0:T(8,128)S(1)} collective-permute-done((f32[2,8,128]{2,1,0:T(8,128)S(1)}, f32[2,8,128]{2,1,0:T(8,128)S(1)}, u32[]{:S(2)}, u32[]{:S(2)}) %collective-permute-start.1) | collective-permute-done | bytes 8224 | tf_op jit(solution)/shard_map/ppermute | solution.py:504
  10.0 0.0 copy-done.1
  10.0 0.0 copy-done
  10.1 18.8 %all_to_all.15.own = f32[8,10,8,128]{3,2,1,0:T(8,128)S(1)} all-to-all(f32[8,10,8,128]{3,2,1,0:T(8,128)S(1)} %bitcast.14), channel_id=1, replica_groups=mesh['gx_0'=12,'gx_1'=2,'gy'=4,'gz'=8] {'gx_1','gy'}, dimensions={0} | all-to-all | bytes 655360 | tf_op jit(solution)/shard_map/all_to_all | solution.py:509
  28.9 0.1 messages.1
  29.0 1.3 %collective-permute-start.2 = (f32[64,8,128]{2,1,0:T(8,128)S(1)}, f32[64,8,128]{2,1,0:T(8,128)S(1)}, u32[]{:S(2)}, u32[]{:S(2)}) collective-permute-start(f32[64,8,128]{2,1,0:T(8,128)S(1)} %get-tuple-element.17), channel_id=1, source_target_pairs={{0,64},{64,128},{128,192},{192,256},{256,320},{320,384},{384,448},... | collective-permute-start | bytes 786440 | tf_op jit(solution)/shard_map/ppermute | solution.py:511
  30.3 1.3 %collective-permute-start.3 = (f32[64,8,128]{2,1,0:T(8,128)S(1)}, f32[64,8,128]{2,1,0:T(8,128)S(1)}, u32[]{:S(2)}, u32[]{:S(2)}) collective-permute-start(f32[64,8,128]{2,1,0:T(8,128)S(1)} %get-tuple-element.18), channel_id=1, source_target_pairs={{64,0},{128,64},{192,128},{256,192},{320,256},{384,320},{448,384},... | collective-permute-start | bytes 786440 | tf_op jit(solution)/shard_map/ppermute | solution.py:512
  31.6 2.3 %collective-permute-start.4 = (f32[16,4,8,128]{3,2,1,0:T(8,128)S(1)}, f32[16,4,8,128]{3,2,1,0:T(8,128)S(1)}, u32[]{:S(2)}, u32[]{:S(2)}) collective-permute-start(f32[16,4,8,128]{3,2,1,0:T(8,128)S(1)} %get-tuple-element.19), channel_id=1, source_target_pairs={{32,0},{33,1},{34,2},{35,3},{36,4},{37,5},{38,6},{39,7},{40,8},{41... | collective-permute-start | bytes 786440 | tf_op jit(solution)/shard_map/ppermute | solution.py:513
  33.9 0.1 stack.32.where_ref
  34.0 1.8 %collective-permute-done.2.low = f32[64,8,128]{2,1,0:T(8,128)S(1)} collective-permute-done((f32[64,8,128]{2,1,0:T(8,128)S(1)}, f32[64,8,128]{2,1,0:T(8,128)S(1)}, u32[]{:S(2)}, u32[]{:S(2)}) %collective-permute-start.2) | collective-permute-done | bytes 262176 | tf_op jit(solution)/shard_map/ppermute | solution.py:511
  35.8 3.8 %collective-permute-done.3.high = f32[64,8,128]{2,1,0:T(8,128)S(1)} collective-permute-done((f32[64,8,128]{2,1,0:T(8,128)S(1)}, f32[64,8,128]{2,1,0:T(8,128)S(1)}, u32[]{:S(2)}, u32[]{:S(2)}) %collective-permute-start.3) | collective-permute-done | bytes 262176 | tf_op jit(solution)/shard_map/ppermute | solution.py:512
  39.7 0.0 collective-permute-done.4.residual
  39.7 12.4 %powers.1 = (f32[4,16,32,128]{3,2,1,0:T(8,128)S(1)}, f32[96,8,128]{2,1,0:T(8,128)S(1)}, f32[24,128]{1,0:T(8,128)S(1)}) custom-call(s32[6]{0:T(128)S(1)} %stack.32.where_ref, f32[8,10,8,128]{3,2,1,0:T(8,128)S(1)} %all_to_all.15.own, f32[64,8,128]{2,1,0:T(8,128)S(1)} %collective-permute-done.2.low, f32[64,8,128]{2,1,0:T(8,128)S(1)} %collective-permute-done.3.high, ...), custom_call_target="tpu_custom_call" | custom-call | tf_op jit(solution)/shard_map/powers/pallas_call | solution.py:388
  52.1 3.2 %collective-permute-start.5 = (f32[96,8,128]{2,1,0:T(8,128)S(1)}, f32[96,8,128]{2,1,0:T(8,128)S(1)}, u32[]{:S(2)}, u32[]{:S(2)}) collective-permute-start(f32[96,8,128]{2,1,0:T(8,128)S(1)} %get-tuple-element.21), channel_id=1, source_target_pairs={{0,32},{32,0},{1,33},{33,1},{2,34},{34,2},{3,35},{35,3},{4,36},{36... | collective-permute-start | bytes 1179656 | tf_op jit(solution)/shard_map/ppermute | solution.py:515
  55.2 1.3 %collective-permute-done.5.other = f32[96,8,128]{2,1,0:T(8,128)S(1)} collective-permute-done((f32[96,8,128]{2,1,0:T(8,128)S(1)}, f32[96,8,128]{2,1,0:T(8,128)S(1)}, u32[]{:S(2)}, u32[]{:S(2)}) %collective-permute-start.5) | collective-permute-done | bytes 393248 | tf_op jit(solution)/shard_map/ppermute | solution.py:515
  56.6 1.3 %products.1 = (f32[2,4,8,8,128]{4,3,2,1,0:T(8,128)}, f32[1,128]{1,0:T(1,128)S(1)}) custom-call(s32[6]{0:T(128)S(1)} %stack.32.where_ref, f32[4,16,32,128]{3,2,1,0:T(8,128)S(1)} %get-tuple-element.20.slab, f32[96,8,128]{2,1,0:T(8,128)S(1)} %collective-permute-done.5.other, f32[24,128]{1,0:T(8,128)S(1)} %get-tuple-element.22.sums), custom_call_target="tpu_custom_call" | custom-call | tf_op jit(solution)/shard_map/products/pallas_call | solution.py:409
  57.9 12.7 %all_to_all.16 = f32[16,1,128]{2,1,0:T(1,128)S(1)} all-to-all(f32[16,1,128]{2,1,0:T(1,128)S(1)} %broadcast_in_dim.10), channel_id=1, replica_groups=mesh['gx_0'=12,'gx_1'=2,'gy'=4,'gz'=8] {'gx_1','gz'}, dimensions={0} | all-to-all | bytes 16384 | tf_op jit(solution)/shard_map/all_to_all | solution.py:483
  70.6 23.3 %all_to_all.17.parts_ref = f32[12,1,128]{2,1,0:T(1,128)S(1)} all-to-all(f32[12,1,128]{2,1,0:T(1,128)S(1)} %broadcast_in_dim.11), channel_id=1, replica_groups=mesh['gx_0'=12,'gx_1'=2,'gy'=4,'gz'=8] {'gx_0'}, dimensions={0} | all-to-all | bytes 12288 | tf_op jit(solution)/shard_map/all_to_all | solution.py:483
  93.9 0.7 totals.1
  (8 shorter events, 0.1 us)
Async XLA Ops:
  0.6 9.4 %copy-start.1 = (f32[8,8,128]{2,1,0:T(8,128)S(1)}, f32[8,8,128]{2,1,0:T(8,128)}, u32[]{:S(2)}) copy-start(f32[8,8,128]{2,1,0:T(8,128)} %residual.1) | copy-start | bytes 98308
  1.6 8.4 %copy-start = (f32[8,8,128]{2,1,0:T(8,128)S(1)}, f32[8,8,128]{2,1,0:T(8,128)}, u32[]{:S(2)}) copy-start(f32[8,8,128]{2,1,0:T(8,128)} %direction.1) | copy-start | bytes 98308
  1.6 5.3 %collective-permute-start = (f32[2,8,128]{2,1,0:T(8,128)S(1)}, f32[2,8,128]{2,1,0:T(8,128)S(1)}, u32[]{:S(2)}, u32[]{:S(2)}) collective-permute-start(f32[2,8,128]{2,1,0:T(8,128)S(1)} %get-tuple-element.15), channel_id=1, source_target_pairs={{0,1},{1,2},{2,3},{3,4},{4,5},{5,6},{6,7},{8,9},{9,10},{10,11},{11... | collective-permute-start | bytes 24584 | tf_op jit(solution)/shard_map/ppermute | solution.py:503
  5.6 4.4 %collective-permute-start.1 = (f32[2,8,128]{2,1,0:T(8,128)S(1)}, f32[2,8,128]{2,1,0:T(8,128)S(1)}, u32[]{:S(2)}, u32[]{:S(2)}) collective-permute-start(f32[2,8,128]{2,1,0:T(8,128)S(1)} %get-tuple-element.16), channel_id=1, source_target_pairs={{1,0},{2,1},{3,2},{4,3},{5,4},{6,5},{7,6},{9,8},{10,9},{11,10},{12... | collective-permute-start | bytes 24584 | tf_op jit(solution)/shard_map/ppermute | solution.py:504
  29.0 6.8 %collective-permute-start.2 = (f32[64,8,128]{2,1,0:T(8,128)S(1)}, f32[64,8,128]{2,1,0:T(8,128)S(1)}, u32[]{:S(2)}, u32[]{:S(2)}) collective-permute-start(f32[64,8,128]{2,1,0:T(8,128)S(1)} %get-tuple-element.17), channel_id=1, source_target_pairs={{0,64},{64,128},{128,192},{192,256},{256,320},{320,384},{384,448},... | collective-permute-start | bytes 786440 | tf_op jit(solution)/shard_map/ppermute | solution.py:511
  30.3 9.4 %collective-permute-start.3 = (f32[64,8,128]{2,1,0:T(8,128)S(1)}, f32[64,8,128]{2,1,0:T(8,128)S(1)}, u32[]{:S(2)}, u32[]{:S(2)}) collective-permute-start(f32[64,8,128]{2,1,0:T(8,128)S(1)} %get-tuple-element.18), channel_id=1, source_target_pairs={{64,0},{128,64},{192,128},{256,192},{320,256},{384,320},{448,384},... | collective-permute-start | bytes 786440 | tf_op jit(solution)/shard_map/ppermute | solution.py:512
  31.6 8.1 %collective-permute-start.4 = (f32[16,4,8,128]{3,2,1,0:T(8,128)S(1)}, f32[16,4,8,128]{3,2,1,0:T(8,128)S(1)}, u32[]{:S(2)}, u32[]{:S(2)}) collective-permute-start(f32[16,4,8,128]{3,2,1,0:T(8,128)S(1)} %get-tuple-element.19), channel_id=1, source_target_pairs={{32,0},{33,1},{34,2},{35,3},{36,4},{37,5},{38,6},{39,7},{40,8},{41... | collective-permute-start | bytes 786440 | tf_op jit(solution)/shard_map/ppermute | solution.py:513
  52.1 4.5 %collective-permute-start.5 = (f32[96,8,128]{2,1,0:T(8,128)S(1)}, f32[96,8,128]{2,1,0:T(8,128)S(1)}, u32[]{:S(2)}, u32[]{:S(2)}) collective-permute-start(f32[96,8,128]{2,1,0:T(8,128)S(1)} %get-tuple-element.21), channel_id=1, source_target_pairs={{0,32},{32,0},{1,33},{33,1},{2,34},{34,2},{3,35},{35,3},{4,36},{36... | collective-permute-start | bytes 1179656 | tf_op jit(solution)/shard_map/ppermute | solution.py:515
